TPU v7x, 256 devices: a whole 4x4x8 slice. The times are simulated.
256 devices in a mesh: zero: 16 (over y, x), width: 16 (over z, core).
Axes of the slice: x: 4, y: 4, z: 8, core: 2. Of those that a mesh axis runs over, the one named last changes fastest.
Arguments:
- train_gate: float32 [5120, 13824], P('zero', 'width'), may hold values from -0.125 to 0.125
- drift_gate: float32 [5120, 13824], P('zero', 'width'), may hold values from -0.078125 to 0.078125
- spread_gate: float32 [5120, 13824], P('zero', 'width'), may hold values from -0.078125 to 0.078125
- train_up: float32 [5120, 13824], P('zero', 'width'), may hold values from -0.125 to 0.125
- drift_up: float32 [5120, 13824], P('zero', 'width'), may hold values from -0.078125 to 0.078125
- spread_up: float32 [5120, 13824], P('zero', 'width'), may hold values from -0.078125 to 0.078125
- norm_gain: float32 [5120], P('zero'), may hold values from 0.25 to 1.75
Outputs:
- serving_gate: bfloat16 [5120, 13824], P(None, 'width')
- serving_up: bfloat16 [5120, 13824], P(None, 'width')
- factor_gate: float32 [13824], P('width')
- factor_up: float32 [13824], P('width')
All inputs are finite; a program needn't handle non-finite values. Where the computation divides by a largest or mean magnitude, that divisor is 1e-20 or more.
Results may differ from a plain program's by a relative error of at most 0.001.
Values may be sent and summed in bfloat16 or wider, within the bound.
No kernel may reach another device: no remote copies, remote signals or barrier semaphores. Data moves between devices by JAX's collectives and lax.ppermute only.
A program may use at most 192 MiB of HBM per device.

v0:
```python
import jax
import jax.numpy as jnp
from jax import lax
from jax.sharding import PartitionSpec as P

learn_rate = 0.3
hold_rate = 0.9


def sent_to_all(array, axis):
    count = lax.axis_size(axis)
    return lax.all_to_all(
        jnp.broadcast_to(array[None], (count, *array.shape)), axis, 0, 0, tiled=True
    )


def taken_together(array, axis):
    return sent_to_all(array, axis).max(axis=0)


def together(arrays, axis):
    ends = [0]
    for a in arrays:
        ends.append(ends[-1] + a.size)
    so_far = taken_together(jnp.concatenate([a.ravel() for a in arrays]), axis)
    return tuple((so_far[b:e].reshape(a.shape) for a, b, e in zip(arrays, ends, ends[1:])))


def sent_together(arrays, axis, dim, along):
    both = jnp.concatenate(arrays, axis=along)
    filled, at, outs = (lax.all_gather(both, axis, axis=dim, tiled=True), 0, [])
    for a in arrays:
        outs.append(lax.slice_in_dim(filled, at, at + a.shape[along], axis=along))
        at += a.shape[along]
    return tuple(outs)


def body(train_gate, drift_gate, spread_gate, train_up, drift_up, spread_up, norm_gain):
    hold_gate = hold_rate * drift_gate + spread_gate
    whole_gate = train_gate - learn_rate * hold_gate
    hold_up = hold_rate * drift_up + spread_up
    whole_up = train_up - learn_rate * hold_up
    whole_gained_gate = whole_gate * norm_gain[:, None]
    whole_gained_up = whole_up * norm_gain[:, None]
    factor_gate, factor_up = together(
        (jnp.max(jnp.abs(whole_gained_gate), axis=0), jnp.max(jnp.abs(whole_gained_up), axis=0)),
        "zero",
    )
    narrow_gate, narrow_up = (
        (whole_gained_gate / factor_gate).astype(jnp.bfloat16),
        (whole_gained_up / factor_up).astype(jnp.bfloat16),
    )
    serving_gate, serving_up = sent_together((narrow_gate, narrow_up), "zero", 0, 1)
    return (serving_gate, serving_up, factor_gate, factor_up)


def solution(mesh):
    return jax.shard_map(
        body,
        mesh=mesh,
        in_specs=(
            P("zero", "width"),
            P("zero", "width"),
            P("zero", "width"),
            P("zero", "width"),
            P("zero", "width"),
            P("zero", "width"),
            P("zero"),
        ),
        out_specs=(P(None, "width"), P(None, "width"), P("width"), P("width")),
        check_vma=False,
    )
```

profile of v0, /device:TPU:1, one launch (start us, length us, event | category | flops | bytes accessed | tf_op | source)
XLA Modules:
  0.0 200.9 jit_solution(1440838860592052964)
XLA Ops:
  7.2 0.0 all-gather.2.cloned.1.call-start
  7.2 3.5 %abs_reduce_fusion.1 = (f32[864]{0:T(1024)S(1)}, f32[320,864]{1,0:T(8,128)S(1)}, f32[864]{0:T(1024)S(1)}, f32[320,864]{1,0:T(8,128)S(1)}) fusion(f32[320]{0:T(512)} %param.13, f32[320,864]{1,0:T(8,128)} %param.7, f32[320,864]{1,0:T(8,128)} %param.9, f32[320,864]{1,0:T(8,128)} %param.8, f32[320,864]{1,0:T(8,128)} %param.10, f32[320,864]{1,0:T(8,128)} %param.12, ...), kind=kLoop, calls=%fused_computation.5 | loop fusion | flops 3868992 | bytes 8855552 | tf_op jit(solution)/shard_map/reduce_max | solution.py:46
  10.7 0.1 pad_maximum_fusion.1
  10.8 0.1 broadcast_in_dim.2
  10.9 14.2 %all_to_all.6 = f32[16,1,1728]{2,1,0:T(1,128)S(1)} all-to-all(f32[16,1,1728]{2,1,0:T(1,128)S(1)} %broadcast_in_dim.2), channel_id=1, replica_groups=mesh['zero'=16,'width'=16] {'zero'}, dimensions={0} | all-to-all | bytes 221184 | tf_op jit(solution)/shard_map/all_to_all | solution.py:12
  25.0 0.1 reduce_max.29
  25.1 0.1 fusion.1
  25.2 0.0 copy-start
  25.2 0.0 copy-start.1
  25.2 0.2 divide_convert_fusion
  25.4 0.4 copy-done
  25.8 0.0 copy-done.1
  25.8 1.3 pad_maximum_fusion
  27.1 0.0 all-gather.2.cloned.1.call-update
  27.1 124.9 %all-gather.2.cloned.1.call-done = bf16[5120,1728]{1,0:T(8,128)(2,1)} async-done(((bf16[320,1728]{1,0:T(8,128)(2,1)}), bf16[5120,1728]{1,0:T(8,128)(2,1)}) %all-gather.2.cloned.1.call-update) | async-done | bytes 17694736 | tf_op jit(solution)/shard_map/all_gather | solution.py:31
  151.9 16.7 %fusion = (bf16[5120,864]{1,0:T(8,128)(2,1)}, bf16[5120,864]{1,0:T(8,128)(2,1)}) fusion(bf16[5120,1728]{1,0:T(8,128)(2,1)} %all-gather.2.cloned.1.call-done), kind=kLoop, calls=%fused_computation.8 | loop fusion | bytes 35389440 | tf_op jit(solution)/shard_map/slice | solution.py:33
  168.6 12.7 %copy.23 = bf16[5120,864]{0,1:T(8,128)(2,1)} copy(bf16[5120,864]{1,0:T(8,128)(2,1)} %get-tuple-element.20) | data formatting | bytes 17694720
  181.3 12.7 %copy.22 = bf16[5120,864]{0,1:T(8,128)(2,1)} copy(bf16[5120,864]{1,0:T(8,128)(2,1)} %get-tuple-element.21) | data formatting | bytes 17694720
Async XLA Ops:
  7.2 144.8 %all-gather.2.cloned.1.call-start = ((), (), s32[]{:S(2)}) async-start(), calls=%async_computation.1 | async-start | bytes 19496960 | tf_op jit(solution)/shard_map/all_gather | solution.py:31
  25.2 0.6 copy-start
  25.2 0.6 copy-start.1
Sparse Core Ops, SparseCore 0:
  27.2 124.6 all-gather.1
where the time goes:
time: 202 us; the launch traced here: 201 us
  waiting for transfers between devices  125 us (62%)
  local copies, waits for them, and re-layouts  42.7 us (21%)
  blocking collectives  14.2 us (7%)
  between operations  14.1 us (7%)
  other arithmetic  5.1 us (3%)
    all_gather x1, waiting for transfers between devices, sent_together(): filled, at, outs = (lax.all_gather(both, axis, axis=dim, tiled=True), 0, [])  125 us
    unnamed x6, local copies, waits for them, and re-layouts  25.8 us
    slice x1, local copies, waits for them, and re-layouts, sent_together(): outs.append(lax.slice_in_dim(filled, at, at + a.shape[along], axis=along))  16.7 us
    all_to_all x1, blocking collectives, sent_to_all(): lax.all_to_all(jnp.broadcast_to(array[None], (count, *array.shape)), axis...  14.2 us
  transfers between devices with their start and end apart: 1, of which 1 were waited for; matrix products, arithmetic and copies ran while one was open for 0% of the time, Pallas kernels for 0%

commit v1 on v0

v1 whole, which is shorter than its diff:
```python
import functools

import jax
import jax.numpy as jnp
from jax import lax
from jax.experimental import pallas as pl
from jax.experimental.pallas import tpu as pltpu
from jax.sharding import PartitionSpec as P


learn_rate = 0.3
hold_rate = 0.9


ROWS = 320
COLS = 864
FULL = 256
HALF = 64
QUART = COLS // 4
PIECE = COLS + QUART
CUT = 544
SIDE = 4


def pack_kernel(w_ref, f_ref, o_ref):
    odd = lax.axis_index("zero") % 2
    full_at = pl.multiple_of(odd * HALF, 8)
    half_at = pl.multiple_of((1 - odd) * FULL, 8)
    for at in range(0, COLS, 128):
        n = min(128, COLS - at)
        f = f_ref[:, at : at + n]
        w = w_ref[pl.ds(full_at, FULL), at : at + n] / f
        o_ref[at : at + n, :] = w.T.astype(jnp.bfloat16)
    h = w_ref[pl.ds(half_at, HALF), :] / f_ref[...]
    t = jnp.concatenate([h, h], axis=0).T
    low = lax.broadcasted_iota(jnp.int32, (2 * QUART, 128), 1) < HALF
    keep = jnp.logical_xor(low, odd == 1)
    p = jnp.where(keep, t[: 2 * QUART], t[2 * QUART :]).astype(jnp.bfloat16)
    o_ref[COLS:, :128] = p[:QUART]
    o_ref[COLS:, 128:] = p[QUART:]


def packed(w, f):
    return pl.pallas_call(
        pack_kernel,
        out_shape=jax.ShapeDtypeStruct((PIECE, 256), jnp.bfloat16),
        in_specs=[pl.BlockSpec(memory_space=pltpu.VMEM)] * 2,
        out_specs=pl.BlockSpec(memory_space=pltpu.VMEM),
        compiler_params=pltpu.CompilerParams(vmem_limit_bytes=8 << 20),
        cost_estimate=pl.CostEstimate(flops=4_000_000, bytes_accessed=1_600_000, transcendentals=0),
    )(w, f.reshape(1, COLS))


def tile_of(kx, ky):
    i = lax.axis_index("zero")
    x, y = i % SIDE, i // SIDE
    j = ((y + SIDE - ky) % SIDE) * SIDE + (x + SIDE - kx) % SIDE
    return pl.multiple_of((5 * j + j % 2) // 2 * 128, 128)


def pair_tile(kx, ky):
    i = lax.axis_index("zero")
    x, y = i % SIDE, i // SIDE
    j = ((y + SIDE - ky) % SIDE) * SIDE + (x + SIDE - kx) % SIDE
    return pl.multiple_of((5 * (j // 2) + 2) * 128, 128)


def place_kernel(plan, n_in, first, *refs):
    ins, outs = refs[:n_in], refs[n_in + len(plan) * (not first) :][: len(plan)]
    tiles, sem_full, sem_tile = refs[-3:]
    odd = lax.axis_index("zero") % 2
    done = []
    for (layout, fulls, _), out in zip(plan, outs):
        for key in fulls:
            at = tile_of(*key)
            for r, a, b in layout[key]:
                hi = min(b, COLS)
                if hi > a:
                    c = pltpu.make_async_copy(
                        ins[r].at[pl.ds(0, hi - a), :], out.at[pl.ds(a, hi - a), pl.ds(at, FULL)], sem_full.at[len(done)]
                    )
                    c.start()
                    done.append(c)

    keep = jnp.logical_xor(lax.broadcasted_iota(jnp.int32, (QUART, 128), 1) < HALF, odd == 1)
    n_tiles = 0
    for (layout, _, pairs), out in zip(plan, outs):

        def half(key, lanes):
            r, a, _ = layout[key][-1]
            return ins[r][COLS - a : PIECE - a, lanes].astype(jnp.float32)

        for p, ky in pairs:
            tile = tiles.at[n_tiles]

            def join(kx):
                for b in range(2):
                    lanes = slice(128 * b, 128 * b + 128)
                    one, two = half((2 * p, ky), lanes), half((kx, ky), lanes)
                    top = jnp.where(keep, one, two)
                    low = pltpu.roll(jnp.where(keep, two, one), HALF, 1)
                    tile[QUART * b : QUART * b + QUART, :] = top.astype(jnp.bfloat16)
                    tile[QUART * b + 2 * QUART : QUART * b + 3 * QUART, :] = low.astype(jnp.bfloat16)

            pl.when(odd == 0)(lambda: join(3 - 2 * p))
            pl.when(odd == 1)(lambda: join(1 + 2 * p))
            c = pltpu.make_async_copy(tile, out.at[:, pl.ds(pair_tile(2 * p, ky), 128)], sem_tile.at[n_tiles])
            c.start()
            done.append(c)
            n_tiles += 1
    for c in done:
        c.wait()


def place(jobs):
    refs, plan = [], []
    for _, got, fulls, pairs in jobs:
        layout = {}
        for key in list(fulls) + [(k, ky) for p, ky in pairs for k in (2 * p, 1, 3)]:
            if key not in layout:
                layout[key], at = [], 0
                for part in got[key]:
                    layout[key].append((len(refs), at, at + part.shape[0]))
                    refs.append(part)
                    at += part.shape[0]
        plan.append((layout, tuple(fulls), tuple(pairs)))
    first = jobs[0][0] is None
    olds = [] if first else [j[0] for j in jobs]
    n_tiles = max(1, sum(len(j[3]) for j in jobs))
    n_full = max(1, sum(len(layout[k]) for layout, fulls, _ in plan for k in fulls))
    shape = jax.ShapeDtypeStruct((COLS, ROWS * SIDE * SIDE), jnp.bfloat16)
    return pl.pallas_call(
        functools.partial(place_kernel, plan, len(refs), first),
        out_shape=[shape] * len(jobs),
        in_specs=[pl.BlockSpec(memory_space=pltpu.VMEM)] * len(refs) + [pl.BlockSpec(memory_space=pl.ANY)] * len(olds),
        out_specs=[pl.BlockSpec(memory_space=pl.ANY)] * len(jobs),
        scratch_shapes=[
            pltpu.VMEM((n_tiles, COLS, 128), jnp.bfloat16),
            pltpu.SemaphoreType.DMA((n_full,)),
            pltpu.SemaphoreType.DMA((n_tiles,)),
        ],
        input_output_aliases={len(refs) + i: i for i in range(len(olds))},
        compiler_params=pltpu.CompilerParams(vmem_limit_bytes=16 << 20),
        cost_estimate=pl.CostEstimate(flops=1_000_000, bytes_accessed=4_000_000, transcendentals=0),
    )(*refs, *olds)


def shift(a, dx, dy):
    pairs = [
        (SIDE * y + x, SIDE * ((y + dy) % SIDE) + (x + dx) % SIDE) for y in range(SIDE) for x in range(SIDE)
    ]
    return lax.ppermute(a, "zero", pairs)


ORDER = [
    *"gs+0 gs-0 us+0 us-0".split(),
    *"ub+0 gb+0 ub-0 gb-0".split(),
    *"gt+1 gt-3 ut+1 ut-3".split(),
    *"ub+1 ub-3 gb+1 gb-3".split(),
    *"ub+3 gb+3".split(),
    *"ub-2a gb-2a ub-2b gb-2b".split(),
    *"ub+2a gb+2a ub+2b gb+2b".split(),
    *"ub-1 gb-1".split(),
    *"Pg0 Pu0".split(),
    *"uf+0 gf+0 uf-3 gf-3".split(),
    *"uf+1 gf+1 uf-2a gf-2a".split(),
    *"uf-2b gf-2b".split(),
    *"Pg1 Pu1 Pg3 Pu3".split(),
    *"Pg2 Pu2".split(),
    *"Pend".split(),
]


def spread(gate, up):
    small = {"g": {"0": gate}, "u": {"0": up}}
    large = {"g": {}, "u": {}}
    out = {"g": None, "u": None}

    def move(a, on_x, sign):
        d = 1 if sign == "+" else -1
        return shift(a, d, 0) if on_x else shift(a, 0, d)

    def pieces(m):
        parts = lambda get: {k: [get(q) for q in ("2a", "2b")] if k == 2 else [get(str(k))] for k in range(SIDE)}
        got = {}
        for step in range(SIDE):
            from_step = (lambda q: small[m][q]) if step == 0 else (lambda q: large[m].get((step, q)))
            for k, v in parts(from_step).items():
                got[(k, step) if m == "g" else (step, k)] = v
        return got

    def put(*jobs):
        res = place([(out[m], pieces(m), fulls, pairs) for m, fulls, pairs in jobs])
        for (m, _, _), r in zip(jobs, res):
            out[m] = r

    every = range(SIDE)
    kernels = {
        "Pg0": [("g", [(k, 0) for k in every], [(0, 0), (1, 0)])],
        "Pg1": [("g", [(k, 1) for k in every], [(0, 1), (1, 1)])],
        "Pg3": [("g", [(k, 3) for k in every], [(0, 3), (1, 3)])],
        "Pg2": [("g", [(0, 2), (3, 2)], [])],
        "Pu0": [("u", [(0, k) for k in every], [])],
        "Pu1": [("u", [(1, k) for k in every], [])],
        "Pu3": [("u", [(3, k) for k in every], [(0, k) for k in every])],
        "Pu2": [("u", [(2, 0), (2, 3)], [(1, 0), (1, 3)])],
        "Pend": [
            ("g", [(1, 2), (2, 2)], [(0, 2), (1, 2)]),
            ("u", [(2, 1), (2, 2)], [(1, 1), (1, 2)]),
        ],
    }
    for name in ORDER:
        if name[0] == "P":
            put(*kernels[name])
            continue
        m, kind, sign, q = name[0], name[1], name[2], name[3:]
        on_x = (m == "g") == (kind in "st")
        step = 1 if sign == "+" else 3
        if kind == "s":
            small[m][str(step)] = move(small[m]["0"], on_x, sign)
        elif kind == "t":
            part = small[m][q][:CUT] if sign == "+" else small[m][q][CUT:]
            small[m]["2a" if sign == "+" else "2b"] = move(part, on_x, sign)
        elif kind == "b":
            large[m][(step, q)] = move(small[m][q], on_x, sign)
        else:
            large[m][(2, q)] = move(large[m][(step, q)], on_x, sign)
    return out["g"], out["u"]


def sent_to_all(array, axis):
    count = lax.axis_size(axis)
    return lax.all_to_all(jnp.broadcast_to(array[None], (count, *array.shape)), axis, 0, 0, tiled=True)


def body(train_gate, drift_gate, spread_gate, train_up, drift_up, spread_up, norm_gain):
    hold_gate = hold_rate * drift_gate + spread_gate
    whole_gate = train_gate - learn_rate * hold_gate
    hold_up = hold_rate * drift_up + spread_up
    whole_up = train_up - learn_rate * hold_up
    gained_gate = whole_gate * norm_gain[:, None]
    gained_up = whole_up * norm_gain[:, None]
    tops = jnp.concatenate([jnp.max(jnp.abs(gained_gate), axis=0), jnp.max(jnp.abs(gained_up), axis=0)])
    tops = sent_to_all(tops, "zero").max(axis=0)
    factor_gate, factor_up = tops[:COLS], tops[COLS:]

    gate = packed(gained_gate, factor_gate)
    up = packed(gained_up, factor_up)
    serving_gate, serving_up = spread(gate, up)
    return serving_gate.T, serving_up.T, factor_gate, factor_up


def solution(mesh):
    return jax.shard_map(
        body,
        mesh=mesh,
        in_specs=(P("zero", "width"),) * 6 + (P("zero"),),
        out_specs=(P(None, "width"), P(None, "width"), P("width"), P("width")),
        check_vma=False,
    )
```

time: 202 us -> 147 us (0.73)
  the two profiles are of different devices: /device:TPU:1 before, /device:TPU:128 now
where the time goes in v1:
time: 147 us
  waiting for transfers between devices  61.8 us (42%)
  starting transfers between devices  52.6 us (36%)
  blocking collectives  14.7 us (10%)
  Pallas kernels  12.7 us (9%)
  other arithmetic  3.65 us (2%)
    ppermute x38, waiting for transfers between devices, shift(): return lax.ppermute(a, 'zero', pairs)  61.8 us
    ppermute x38, starting transfers between devices, shift(): return lax.ppermute(a, 'zero', pairs)  52.6 us
    all_to_all x1, blocking collectives, sent_to_all(): lax.all_to_all(jnp.broadcast_to(array[None], (count, *array.shape)), axis...  14.7 us
    pallas_call x9, Pallas kernels, place(): pl.pallas_call(functools.partial(place_kernel, plan, len(refs), first), o...  12.2 us
    reduce_max x1, other arithmetic, body(): jnp.max(jnp.abs(gained_up), axis=0)  3.49 us
  transfers between devices with their start and end apart: 38, of which 15 were waited for; matrix products, arithmetic and copies ran while one was open for 0% of the time, Pallas kernels for 7%

profile of v1, /device:TPU:128, one launch (start us, length us, event | category | flops | bytes accessed | tf_op | source)
XLA Modules:
  0.0 146.7 jit_solution(7997131423384781223)
XLA Ops:
  0.6 3.5 %abs_reduce_fusion = (f32[864]{0:T(1024)S(1)}, f32[320,864]{1,0:T(8,128)S(1)}, f32[864]{0:T(1024)S(1)}, f32[320,864]{1,0:T(8,128)S(1)}) fusion(f32[320]{0:T(512)} %param.13, f32[320,864]{1,0:T(8,128)} %param.10, f32[320,864]{1,0:T(8,128)} %param.12, f32[320,864]{1,0:T(8,128)} %param.11, f32[320,864]{1,0:T(8,128)} %param.7, f32[320,864]{1,0:T(8,128)} %param.9, ...), kind=kLoop, calls=%fused_computation | loop fusion | flops 3868992 | bytes 8855552 | tf_op jit(solution)/shard_map/reduce_max | solution.py:243
  4.3 14.7 %all_to_all.6 = f32[16,1,1728]{2,1,0:T(1,128)S(1)} all-to-all(f32[16,1,1728]{2,1,0:T(1,128)S(1)} %broadcast_in_dim.2), channel_id=1, replica_groups=mesh['zero'=16,'width'=16] {'zero'}, dimensions={0} | all-to-all | bytes 221184 | tf_op jit(solution)/shard_map/all_to_all | solution.py:233
  22.5 2.7 %collective-permute-start.6 = (bf16[1080,256]{1,0:T(8,128)(2,1)S(1)}, bf16[1080,256]{1,0:T(8,128)(2,1)S(1)}, u32[]{:S(2)}, u32[]{:S(2)}) collective-permute-start(bf16[1080,256]{1,0:T(8,128)(2,1)S(1)} %shard_map.102.refs_0_), channel_id=1, source_target_pairs={{0,48},{16,0},{32,16},{48,32},{64,112},{80,64},{96,80},{112,96},{1... | collective-permute-start | bytes 1658888 | tf_op jit(solution)/shard_map/ppermute | solution.py:152
  25.2 2.1 %collective-permute-start.20 = (bf16[1080,256]{1,0:T(8,128)(2,1)S(1)}, bf16[1080,256]{1,0:T(8,128)(2,1)S(1)}, u32[]{:S(2)}, u32[]{:S(2)}) collective-permute-start(bf16[1080,256]{1,0:T(8,128)(2,1)S(1)} %shard_map.103.refs_0_.refs_5_), channel_id=1, source_target_pairs={{0,192},{16,208},{32,224},{48,240},{64,0},{80,16},{96,32},{112,48}... | collective-permute-start | bytes 1658888 | tf_op jit(solution)/shard_map/ppermute | solution.py:152
  27.3 7.6 %collective-permute-done.27.refs_0_ = bf16[1080,256]{1,0:T(8,128)(2,1)S(1)} collective-permute-done((bf16[1080,256]{1,0:T(8,128)(2,1)S(1)}, bf16[1080,256]{1,0:T(8,128)(2,1)S(1)}, u32[]{:S(2)}, u32[]{:S(2)}) %collective-permute-start.27) | collective-permute-done | bytes 552992 | tf_op jit(solution)/shard_map/ppermute | solution.py:152
  37.6 1.6 %collective-permute-start.3 = (bf16[544,256]{1,0:T(8,128)(2,1)S(1)}, bf16[544,256]{1,0:T(8,128)(2,1)S(1)}, u32[]{:S(2)}, u32[]{:S(2)}) collective-permute-start(bf16[544,256]{1,0:T(8,128)(2,1)S(1)} %slice.25), channel_id=1, source_target_pairs={{0,16},{16,32},{32,48},{48,0},{64,80},{80,96},{96,112},{112,64},{1... | collective-permute-start | bytes 835592 | tf_op jit(solution)/shard_map/ppermute | solution.py:152
  39.2 5.1 %collective-permute-done.20.refs_4_.refs_13_ = bf16[1080,256]{1,0:T(8,128)(2,1)S(1)} collective-permute-done((bf16[1080,256]{1,0:T(8,128)(2,1)S(1)}, bf16[1080,256]{1,0:T(8,128)(2,1)S(1)}, u32[]{:S(2)}, u32[]{:S(2)}) %collective-permute-start.20) | collective-permute-done | bytes 552992 | tf_op jit(solution)/shard_map/ppermute | solution.py:152
  44.6 3.6 %collective-permute-done.10.refs_0_ = bf16[1080,256]{1,0:T(8,128)(2,1)S(1)} collective-permute-done((bf16[1080,256]{1,0:T(8,128)(2,1)S(1)}, bf16[1080,256]{1,0:T(8,128)(2,1)S(1)}, u32[]{:S(2)}, u32[]{:S(2)}) %collective-permute-start.10) | collective-permute-done | bytes 552992 | tf_op jit(solution)/shard_map/ppermute | solution.py:152
  48.3 4.0 %collective-permute-start.7 = (bf16[536,256]{1,0:T(8,128)(2,1)S(1)}, bf16[536,256]{1,0:T(8,128)(2,1)S(1)}, u32[]{:S(2)}, u32[]{:S(2)}) collective-permute-start(bf16[536,256]{1,0:T(8,128)(2,1)S(1)} %slice.26), channel_id=1, source_target_pairs={{0,48},{16,0},{32,16},{48,32},{64,112},{80,64},{96,80},{112,96},{1... | collective-permute-start | bytes 823304 | tf_op jit(solution)/shard_map/ppermute | solution.py:152
  52.3 2.0 %collective-permute-start.11 = (bf16[1080,256]{1,0:T(8,128)(2,1)S(1)}, bf16[1080,256]{1,0:T(8,128)(2,1)S(1)}, u32[]{:S(2)}, u32[]{:S(2)}) collective-permute-start(bf16[1080,256]{1,0:T(8,128)(2,1)S(1)} %collective-permute-done.10.refs_0_), channel_id=1, source_target_pairs={{0,64},{16,80},{32,96},{48,112},{64,128},{80,144},{96,160},{112,17... | collective-permute-start | bytes 1658888 | tf_op jit(solution)/shard_map/ppermute | solution.py:152
  54.3 2.0 %collective-permute-done.7.refs_3_ = bf16[536,256]{1,0:T(8,128)(2,1)S(1)} collective-permute-done((bf16[536,256]{1,0:T(8,128)(2,1)S(1)}, bf16[536,256]{1,0:T(8,128)(2,1)S(1)}, u32[]{:S(2)}, u32[]{:S(2)}) %collective-permute-start.7) | collective-permute-done | bytes 274464 | tf_op jit(solution)/shard_map/ppermute | solution.py:152
  56.4 3.8 %collective-permute-done.21.refs_3_.refs_10_ = bf16[536,256]{1,0:T(8,128)(2,1)S(1)} collective-permute-done((bf16[536,256]{1,0:T(8,128)(2,1)S(1)}, bf16[536,256]{1,0:T(8,128)(2,1)S(1)}, u32[]{:S(2)}, u32[]{:S(2)}) %collective-permute-start.21) | collective-permute-done | bytes 274464 | tf_op jit(solution)/shard_map/ppermute | solution.py:152
  60.3 2.7 %collective-permute-start.8 = (bf16[536,256]{1,0:T(8,128)(2,1)S(1)}, bf16[536,256]{1,0:T(8,128)(2,1)S(1)}, u32[]{:S(2)}, u32[]{:S(2)}) collective-permute-start(bf16[536,256]{1,0:T(8,128)(2,1)S(1)} %collective-permute-done.7.refs_3_), channel_id=1, source_target_pairs={{0,192},{16,208},{32,224},{48,240},{64,0},{80,16},{96,32},{112,48}... | collective-permute-start | bytes 823304 | tf_op jit(solution)/shard_map/ppermute | solution.py:152
  62.9 3.2 %collective-permute-start.22 = (bf16[536,256]{1,0:T(8,128)(2,1)S(1)}, bf16[536,256]{1,0:T(8,128)(2,1)S(1)}, u32[]{:S(2)}, u32[]{:S(2)}) collective-permute-start(bf16[536,256]{1,0:T(8,128)(2,1)S(1)} %collective-permute-done.21.refs_3_.refs_10_), channel_id=1, source_target_pairs={{0,48},{16,0},{32,16},{48,32},{64,112},{80,64},{96,80},{112,96},{1... | collective-permute-start | bytes 823304 | tf_op jit(solution)/shard_map/ppermute | solution.py:152
  66.2 4.8 %collective-permute-done.30.refs_3_ = bf16[536,256]{1,0:T(8,128)(2,1)S(1)} collective-permute-done((bf16[536,256]{1,0:T(8,128)(2,1)S(1)}, bf16[536,256]{1,0:T(8,128)(2,1)S(1)}, u32[]{:S(2)}, u32[]{:S(2)}) %collective-permute-start.30) | collective-permute-done | bytes 274464 | tf_op jit(solution)/shard_map/ppermute | solution.py:152
  71.8 2.4 %collective-permute-start.12 = (bf16[1080,256]{1,0:T(8,128)(2,1)S(1)}, bf16[1080,256]{1,0:T(8,128)(2,1)S(1)}, u32[]{:S(2)}, u32[]{:S(2)}) collective-permute-start(bf16[1080,256]{1,0:T(8,128)(2,1)S(1)} %collective-permute-done.6.refs_4_), channel_id=1, source_target_pairs={{0,192},{16,208},{32,224},{48,240},{64,0},{80,16},{96,32},{112,48}... | collective-permute-start | bytes 1658888 | tf_op jit(solution)/shard_map/ppermute | solution.py:152
  74.3 1.9 %collective-permute-start.1 = (bf16[1080,256]{1,0:T(8,128)(2,1)S(1)}, bf16[1080,256]{1,0:T(8,128)(2,1)S(1)}, u32[]{:S(2)}, u32[]{:S(2)}) collective-permute-start(bf16[1080,256]{1,0:T(8,128)(2,1)S(1)} %collective-permute-done.refs_1_), channel_id=1, source_target_pairs={{0,64},{16,80},{32,96},{48,112},{64,128},{80,144},{96,160},{112,17... | collective-permute-start | bytes 1658888 | tf_op jit(solution)/shard_map/ppermute | solution.py:152
  76.6 11.0 %collective-permute-done.31.refs_4_ = bf16[1080,256]{1,0:T(8,128)(2,1)S(1)} collective-permute-done((bf16[1080,256]{1,0:T(8,128)(2,1)S(1)}, bf16[1080,256]{1,0:T(8,128)(2,1)S(1)}, u32[]{:S(2)}, u32[]{:S(2)}) %collective-permute-start.31) | collective-permute-done | bytes 552992 | tf_op jit(solution)/shard_map/ppermute | solution.py:152
  87.9 2.9 %collective-permute-start.34 = (bf16[1080,256]{1,0:T(8,128)(2,1)S(1)}, bf16[1080,256]{1,0:T(8,128)(2,1)S(1)}, u32[]{:S(2)}, u32[]{:S(2)}) collective-permute-start(bf16[1080,256]{1,0:T(8,128)(2,1)S(1)} %collective-permute-done.20.refs_4_.refs_13_), channel_id=1, source_target_pairs={{0,48},{16,0},{32,16},{48,32},{64,112},{80,64},{96,80},{112,96},{1... | collective-permute-start | bytes 1658888 | tf_op jit(solution)/shard_map/ppermute | solution.py:152
  90.8 2.5 %collective-permute-done.28.refs_1_ = bf16[1080,256]{1,0:T(8,128)(2,1)S(1)} collective-permute-done((bf16[1080,256]{1,0:T(8,128)(2,1)S(1)}, bf16[1080,256]{1,0:T(8,128)(2,1)S(1)}, u32[]{:S(2)}, u32[]{:S(2)}) %collective-permute-start.28) | collective-permute-done | bytes 552992 | tf_op jit(solution)/shard_map/ppermute | solution.py:152
  93.3 2.6 %collective-permute-start.24 = (bf16[1080,256]{1,0:T(8,128)(2,1)S(1)}, bf16[1080,256]{1,0:T(8,128)(2,1)S(1)}, u32[]{:S(2)}, u32[]{:S(2)}) collective-permute-start(bf16[1080,256]{1,0:T(8,128)(2,1)S(1)} %collective-permute-done.14.refs_1_.refs_7_), channel_id=1, source_target_pairs={{0,48},{16,0},{32,16},{48,32},{64,112},{80,64},{96,80},{112,96},{1... | collective-permute-start | bytes 1658888 | tf_op jit(solution)/shard_map/ppermute | solution.py:152
  96.7 6.3 %collective-permute-done.37.refs_4_.refs_14_ = bf16[1080,256]{1,0:T(8,128)(2,1)S(1)} collective-permute-done((bf16[1080,256]{1,0:T(8,128)(2,1)S(1)}, bf16[1080,256]{1,0:T(8,128)(2,1)S(1)}, u32[]{:S(2)}, u32[]{:S(2)}) %collective-permute-start.37) | collective-permute-done | bytes 552992 | tf_op jit(solution)/shard_map/ppermute | solution.py:152
  103.4 5.8 %collective-permute-done.24.refs_1_.refs_9_ = bf16[1080,256]{1,0:T(8,128)(2,1)S(1)} collective-permute-done((bf16[1080,256]{1,0:T(8,128)(2,1)S(1)}, bf16[1080,256]{1,0:T(8,128)(2,1)S(1)}, u32[]{:S(2)}, u32[]{:S(2)}) %collective-permute-start.24) | collective-permute-done | bytes 552992 | tf_op jit(solution)/shard_map/ppermute | solution.py:152
  109.3 3.7 %collective-permute-start.13 = (bf16[1080,256]{1,0:T(8,128)(2,1)S(1)}, bf16[1080,256]{1,0:T(8,128)(2,1)S(1)}, u32[]{:S(2)}, u32[]{:S(2)}) collective-permute-start(bf16[1080,256]{1,0:T(8,128)(2,1)S(1)} %collective-permute-done.12.refs_4_), channel_id=1, source_target_pairs={{0,192},{16,208},{32,224},{48,240},{64,0},{80,16},{96,32},{112,48}... | collective-permute-start | bytes 1658888 | tf_op jit(solution)/shard_map/ppermute | solution.py:152
  113.6 3.1 %collective-permute-start.18 = (bf16[544,256]{1,0:T(8,128)(2,1)S(1)}, bf16[544,256]{1,0:T(8,128)(2,1)S(1)}, u32[]{:S(2)}, u32[]{:S(2)}) collective-permute-start(bf16[544,256]{1,0:T(8,128)(2,1)S(1)} %collective-permute-done.17.refs_2_.refs_9_), channel_id=1, source_target_pairs={{0,48},{16,0},{32,16},{48,32},{64,112},{80,64},{96,80},{112,96},{1... | collective-permute-start | bytes 835592 | tf_op jit(solution)/shard_map/ppermute | solution.py:152
  117.1 1.7 %collective-permute-start.2 = (bf16[1080,256]{1,0:T(8,128)(2,1)S(1)}, bf16[1080,256]{1,0:T(8,128)(2,1)S(1)}, u32[]{:S(2)}, u32[]{:S(2)}) collective-permute-start(bf16[1080,256]{1,0:T(8,128)(2,1)S(1)} %collective-permute-done.1.refs_1_), channel_id=1, source_target_pairs={{0,64},{16,80},{32,96},{48,112},{64,128},{80,144},{96,160},{112,17... | collective-permute-start | bytes 1658888 | tf_op jit(solution)/shard_map/ppermute | solution.py:152
  118.8 4.3 %collective-permute-done.18.refs_2_.refs_12_ = bf16[544,256]{1,0:T(8,128)(2,1)S(1)} collective-permute-done((bf16[544,256]{1,0:T(8,128)(2,1)S(1)}, bf16[544,256]{1,0:T(8,128)(2,1)S(1)}, u32[]{:S(2)}, u32[]{:S(2)}) %collective-permute-start.18) | collective-permute-done | bytes 278560 | tf_op jit(solution)/shard_map/ppermute | solution.py:152
  124.0 3.9 %collective-permute-done.9.refs_2_ = bf16[536,256]{1,0:T(8,128)(2,1)S(1)} collective-permute-done((bf16[536,256]{1,0:T(8,128)(2,1)S(1)}, bf16[536,256]{1,0:T(8,128)(2,1)S(1)}, u32[]{:S(2)}, u32[]{:S(2)}) %collective-permute-start.9) | collective-permute-done | bytes 274464 | tf_op jit(solution)/shard_map/ppermute | solution.py:152
  127.9 3.7 %collective-permute-start.5 = (bf16[544,256]{1,0:T(8,128)(2,1)S(1)}, bf16[544,256]{1,0:T(8,128)(2,1)S(1)}, u32[]{:S(2)}, u32[]{:S(2)}) collective-permute-start(bf16[544,256]{1,0:T(8,128)(2,1)S(1)} %collective-permute-done.4.refs_2_), channel_id=1, source_target_pairs={{0,192},{16,208},{32,224},{48,240},{64,0},{80,16},{96,32},{112,48}... | collective-permute-start | bytes 835592 | tf_op jit(solution)/shard_map/ppermute | solution.py:152
  132.8 1.4 collective-permute-start.23
  141.1 1.6 %shard_map.110.refs_6_ = bf16[864,5120]{1,0:T(8,128)(2,1)} custom-call(bf16[1080,256]{1,0:T(8,128)(2,1)S(1)} %collective-permute-done.36.refs_0_.refs_3_, bf16[1080,256]{1,0:T(8,128)(2,1)S(1)} %collective-permute-done.24.refs_1_.refs_9_, bf16[544,256]{1,0:T(8,128)(2,1)S(1)} %collective-permute-done.18.refs_2_.refs_12_, ...), custom_call_target="tpu_custom_call", output_to_operand_aliasing={{}: (15, {})} | custom-call | flops 1000000 | bytes 4000000 | tf_op jit(solution)/shard_map/pallas_call | solution.py:132
  144.9 1.6 %shard_map.112 = (bf16[864,5120]{1,0:T(8,128)(2,1)}, bf16[864,5120]{1,0:T(8,128)(2,1)}) custom-call(bf16[1080,256]{1,0:T(8,128)(2,1)S(1)} %collective-permute-done.2.refs_0_, bf16[544,256]{1,0:T(8,128)(2,1)S(1)} %collective-permute-done.5.refs_1_, ...), custom_call_target="tpu_custom_call", output_to_operand_aliasing={{0}: (14, {}), {1}: (15, {})} | custom-call | flops 1000000 | bytes 4000000 | tf_op jit(solution)/shard_map/pallas_call | solution.py:132
  (71 shorter events, 21.6 us)
Async XLA Ops:
  19.4 15.5 %collective-permute-start.27 = (bf16[1080,256]{1,0:T(8,128)(2,1)S(1)}, bf16[1080,256]{1,0:T(8,128)(2,1)S(1)}, u32[]{:S(2)}, u32[]{:S(2)}) collective-permute-start(bf16[1080,256]{1,0:T(8,128)(2,1)S(1)} %shard_map.102.refs_0_), channel_id=1, source_target_pairs={{0,192},{16,208},{32,224},{48,240},{64,0},{80,16},{96,32},{112,48}... | collective-permute-start | bytes 1658888 | tf_op jit(solution)/shard_map/ppermute | solution.py:152
  20.4 14.8 %collective-permute-start = (bf16[1080,256]{1,0:T(8,128)(2,1)S(1)}, bf16[1080,256]{1,0:T(8,128)(2,1)S(1)}, u32[]{:S(2)}, u32[]{:S(2)}) collective-permute-start(bf16[1080,256]{1,0:T(8,128)(2,1)S(1)} %shard_map.102.refs_0_), channel_id=1, source_target_pairs={{0,16},{16,32},{32,48},{48,0},{64,80},{80,96},{96,112},{112,64},{1... | collective-permute-start | bytes 1658888 | tf_op jit(solution)/shard_map/ppermute | solution.py:152
  21.3 15.2 %collective-permute-start.14 = (bf16[1080,256]{1,0:T(8,128)(2,1)S(1)}, bf16[1080,256]{1,0:T(8,128)(2,1)S(1)}, u32[]{:S(2)}, u32[]{:S(2)}) collective-permute-start(bf16[1080,256]{1,0:T(8,128)(2,1)S(1)} %shard_map.103.refs_0_.refs_5_), channel_id=1, source_target_pairs={{0,64},{16,80},{32,96},{48,112},{64,128},{80,144},{96,160},{112,17... | collective-permute-start | bytes 1658888 | tf_op jit(solution)/shard_map/ppermute | solution.py:152
  22.5 15.1 %collective-permute-start.6 = (bf16[1080,256]{1,0:T(8,128)(2,1)S(1)}, bf16[1080,256]{1,0:T(8,128)(2,1)S(1)}, u32[]{:S(2)}, u32[]{:S(2)}) collective-permute-start(bf16[1080,256]{1,0:T(8,128)(2,1)S(1)} %shard_map.102.refs_0_), channel_id=1, source_target_pairs={{0,48},{16,0},{32,16},{48,32},{64,112},{80,64},{96,80},{112,96},{1... | collective-permute-start | bytes 1658888 | tf_op jit(solution)/shard_map/ppermute | solution.py:152
  25.2 19.1 %collective-permute-start.20 = (bf16[1080,256]{1,0:T(8,128)(2,1)S(1)}, bf16[1080,256]{1,0:T(8,128)(2,1)S(1)}, u32[]{:S(2)}, u32[]{:S(2)}) collective-permute-start(bf16[1080,256]{1,0:T(8,128)(2,1)S(1)} %shard_map.103.refs_0_.refs_5_), channel_id=1, source_target_pairs={{0,192},{16,208},{32,224},{48,240},{64,0},{80,16},{96,32},{112,48}... | collective-permute-start | bytes 1658888 | tf_op jit(solution)/shard_map/ppermute | solution.py:152
  34.9 13.3 %collective-permute-start.10 = (bf16[1080,256]{1,0:T(8,128)(2,1)S(1)}, bf16[1080,256]{1,0:T(8,128)(2,1)S(1)}, u32[]{:S(2)}, u32[]{:S(2)}) collective-permute-start(bf16[1080,256]{1,0:T(8,128)(2,1)S(1)} %shard_map.102.refs_0_), channel_id=1, source_target_pairs={{0,64},{16,80},{32,96},{48,112},{64,128},{80,144},{96,160},{112,17... | collective-permute-start | bytes 1658888 | tf_op jit(solution)/shard_map/ppermute | solution.py:152
  35.3 17.0 %collective-permute-start.36 = (bf16[1080,256]{1,0:T(8,128)(2,1)S(1)}, bf16[1080,256]{1,0:T(8,128)(2,1)S(1)}, u32[]{:S(2)}, u32[]{:S(2)}) collective-permute-start(bf16[1080,256]{1,0:T(8,128)(2,1)S(1)} %shard_map.103.refs_0_.refs_5_), channel_id=1, source_target_pairs={{0,48},{16,0},{32,16},{48,32},{64,112},{80,64},{96,80},{112,96},{1... | collective-permute-start | bytes 1658888 | tf_op jit(solution)/shard_map/ppermute | solution.py:152
  36.5 15.8 %collective-permute-start.32 = (bf16[1080,256]{1,0:T(8,128)(2,1)S(1)}, bf16[1080,256]{1,0:T(8,128)(2,1)S(1)}, u32[]{:S(2)}, u32[]{:S(2)}) collective-permute-start(bf16[1080,256]{1,0:T(8,128)(2,1)S(1)} %shard_map.103.refs_0_.refs_5_), channel_id=1, source_target_pairs={{0,16},{16,32},{32,48},{48,0},{64,80},{80,96},{96,112},{112,64},{1... | collective-permute-start | bytes 1658888 | tf_op jit(solution)/shard_map/ppermute | solution.py:152
  37.6 25.4 %collective-permute-start.3 = (bf16[544,256]{1,0:T(8,128)(2,1)S(1)}, bf16[544,256]{1,0:T(8,128)(2,1)S(1)}, u32[]{:S(2)}, u32[]{:S(2)}) collective-permute-start(bf16[544,256]{1,0:T(8,128)(2,1)S(1)} %slice.25), channel_id=1, source_target_pairs={{0,16},{16,32},{32,48},{48,0},{64,80},{80,96},{96,112},{112,64},{1... | collective-permute-start | bytes 835592 | tf_op jit(solution)/shard_map/ppermute | solution.py:152
  44.3 18.6 %collective-permute-start.17 = (bf16[544,256]{1,0:T(8,128)(2,1)S(1)}, bf16[544,256]{1,0:T(8,128)(2,1)S(1)}, u32[]{:S(2)}, u32[]{:S(2)}) collective-permute-start(bf16[544,256]{1,0:T(8,128)(2,1)S(1)} %slice.28), channel_id=1, source_target_pairs={{0,64},{16,80},{32,96},{48,112},{64,128},{80,144},{96,160},{112,17... | collective-permute-start | bytes 835592 | tf_op jit(solution)/shard_map/ppermute | solution.py:152
  52.3 23.9 %collective-permute-start.11 = (bf16[1080,256]{1,0:T(8,128)(2,1)S(1)}, bf16[1080,256]{1,0:T(8,128)(2,1)S(1)}, u32[]{:S(2)}, u32[]{:S(2)}) collective-permute-start(bf16[1080,256]{1,0:T(8,128)(2,1)S(1)} %collective-permute-done.10.refs_0_), channel_id=1, source_target_pairs={{0,64},{16,80},{32,96},{48,112},{64,128},{80,144},{96,160},{112,17... | collective-permute-start | bytes 1658888 | tf_op jit(solution)/shard_map/ppermute | solution.py:152
  56.3 14.7 %collective-permute-start.30 = (bf16[536,256]{1,0:T(8,128)(2,1)S(1)}, bf16[536,256]{1,0:T(8,128)(2,1)S(1)}, u32[]{:S(2)}, u32[]{:S(2)}) collective-permute-start(bf16[536,256]{1,0:T(8,128)(2,1)S(1)} %collective-permute-done.7.refs_3_), channel_id=1, source_target_pairs={{0,64},{16,80},{32,96},{48,112},{64,128},{80,144},{96,160},{112,17... | collective-permute-start | bytes 823304 | tf_op jit(solution)/shard_map/ppermute | solution.py:152
  60.3 11.6 %collective-permute-start.8 = (bf16[536,256]{1,0:T(8,128)(2,1)S(1)}, bf16[536,256]{1,0:T(8,128)(2,1)S(1)}, u32[]{:S(2)}, u32[]{:S(2)}) collective-permute-start(bf16[536,256]{1,0:T(8,128)(2,1)S(1)} %collective-permute-done.7.refs_3_), channel_id=1, source_target_pairs={{0,192},{16,208},{32,224},{48,240},{64,0},{80,16},{96,32},{112,48}... | collective-permute-start | bytes 823304 | tf_op jit(solution)/shard_map/ppermute | solution.py:152
  71.0 16.6 %collective-permute-start.31 = (bf16[1080,256]{1,0:T(8,128)(2,1)S(1)}, bf16[1080,256]{1,0:T(8,128)(2,1)S(1)}, u32[]{:S(2)}, u32[]{:S(2)}) collective-permute-start(bf16[1080,256]{1,0:T(8,128)(2,1)S(1)} %collective-permute-done.6.refs_4_), channel_id=1, source_target_pairs={{0,64},{16,80},{32,96},{48,112},{64,128},{80,144},{96,160},{112,17... | collective-permute-start | bytes 1658888 | tf_op jit(solution)/shard_map/ppermute | solution.py:152
  71.8 16.1 %collective-permute-start.12 = (bf16[1080,256]{1,0:T(8,128)(2,1)S(1)}, bf16[1080,256]{1,0:T(8,128)(2,1)S(1)}, u32[]{:S(2)}, u32[]{:S(2)}) collective-permute-start(bf16[1080,256]{1,0:T(8,128)(2,1)S(1)} %collective-permute-done.6.refs_4_), channel_id=1, source_target_pairs={{0,192},{16,208},{32,224},{48,240},{64,0},{80,16},{96,32},{112,48}... | collective-permute-start | bytes 1658888 | tf_op jit(solution)/shard_map/ppermute | solution.py:152
  74.2 19.2 %collective-permute-start.28 = (bf16[1080,256]{1,0:T(8,128)(2,1)S(1)}, bf16[1080,256]{1,0:T(8,128)(2,1)S(1)}, u32[]{:S(2)}, u32[]{:S(2)}) collective-permute-start(bf16[1080,256]{1,0:T(8,128)(2,1)S(1)} %collective-permute-done.refs_1_), channel_id=1, source_target_pairs={{0,192},{16,208},{32,224},{48,240},{64,0},{80,16},{96,32},{112,48}... | collective-permute-start | bytes 1658888 | tf_op jit(solution)/shard_map/ppermute | solution.py:152
  74.3 21.6 %collective-permute-start.1 = (bf16[1080,256]{1,0:T(8,128)(2,1)S(1)}, bf16[1080,256]{1,0:T(8,128)(2,1)S(1)}, u32[]{:S(2)}, u32[]{:S(2)}) collective-permute-start(bf16[1080,256]{1,0:T(8,128)(2,1)S(1)} %collective-permute-done.refs_1_), channel_id=1, source_target_pairs={{0,64},{16,80},{32,96},{48,112},{64,128},{80,144},{96,160},{112,17... | collective-permute-start | bytes 1658888 | tf_op jit(solution)/shard_map/ppermute | solution.py:152
  76.2 20.4 %collective-permute-start.33 = (bf16[1080,256]{1,0:T(8,128)(2,1)S(1)}, bf16[1080,256]{1,0:T(8,128)(2,1)S(1)}, u32[]{:S(2)}, u32[]{:S(2)}) collective-permute-start(bf16[1080,256]{1,0:T(8,128)(2,1)S(1)} %collective-permute-done.32.refs_0_.refs_6_.refs_2_), channel_id=1, source_target_pairs={{0,16},{16,32},{32,48},{48,0},{64,80},{80,96},{96,112},{112,64},{1... | collective-permute-start | bytes 1658888 | tf_op jit(solution)/shard_map/ppermute | solution.py:152
  87.6 15.4 %collective-permute-start.37 = (bf16[1080,256]{1,0:T(8,128)(2,1)S(1)}, bf16[1080,256]{1,0:T(8,128)(2,1)S(1)}, u32[]{:S(2)}, u32[]{:S(2)}) collective-permute-start(bf16[1080,256]{1,0:T(8,128)(2,1)S(1)} %collective-permute-done.20.refs_4_.refs_13_), channel_id=1, source_target_pairs={{0,16},{16,32},{32,48},{48,0},{64,80},{80,96},{96,112},{112,64},{1... | collective-permute-start | bytes 1658888 | tf_op jit(solution)/shard_map/ppermute | solution.py:152
  87.9 15.1 %collective-permute-start.34 = (bf16[1080,256]{1,0:T(8,128)(2,1)S(1)}, bf16[1080,256]{1,0:T(8,128)(2,1)S(1)}, u32[]{:S(2)}, u32[]{:S(2)}) collective-permute-start(bf16[1080,256]{1,0:T(8,128)(2,1)S(1)} %collective-permute-done.20.refs_4_.refs_13_), channel_id=1, source_target_pairs={{0,48},{16,0},{32,16},{48,32},{64,112},{80,64},{96,80},{112,96},{1... | collective-permute-start | bytes 1658888 | tf_op jit(solution)/shard_map/ppermute | solution.py:152
  93.3 15.9 %collective-permute-start.24 = (bf16[1080,256]{1,0:T(8,128)(2,1)S(1)}, bf16[1080,256]{1,0:T(8,128)(2,1)S(1)}, u32[]{:S(2)}, u32[]{:S(2)}) collective-permute-start(bf16[1080,256]{1,0:T(8,128)(2,1)S(1)} %collective-permute-done.14.refs_1_.refs_7_), channel_id=1, source_target_pairs={{0,48},{16,0},{32,16},{48,32},{64,112},{80,64},{96,80},{112,96},{1... | collective-permute-start | bytes 1658888 | tf_op jit(solution)/shard_map/ppermute | solution.py:152
  95.9 17.7 %collective-permute-start.15 = (bf16[1080,256]{1,0:T(8,128)(2,1)S(1)}, bf16[1080,256]{1,0:T(8,128)(2,1)S(1)}, u32[]{:S(2)}, u32[]{:S(2)}) collective-permute-start(bf16[1080,256]{1,0:T(8,128)(2,1)S(1)} %collective-permute-done.14.refs_1_.refs_7_), channel_id=1, source_target_pairs={{0,16},{16,32},{32,48},{48,0},{64,80},{80,96},{96,112},{112,64},{1... | collective-permute-start | bytes 1658888 | tf_op jit(solution)/shard_map/ppermute | solution.py:152
  96.7 20.0 %collective-permute-start.29 = (bf16[544,256]{1,0:T(8,128)(2,1)S(1)}, bf16[544,256]{1,0:T(8,128)(2,1)S(1)}, u32[]{:S(2)}, u32[]{:S(2)}) collective-permute-start(bf16[544,256]{1,0:T(8,128)(2,1)S(1)} %collective-permute-done.3.refs_2_), channel_id=1, source_target_pairs={{0,64},{16,80},{32,96},{48,112},{64,128},{80,144},{96,160},{112,17... | collective-permute-start | bytes 835592 | tf_op jit(solution)/shard_map/ppermute | solution.py:152
  102.9 13.9 %collective-permute-start.4 = (bf16[544,256]{1,0:T(8,128)(2,1)S(1)}, bf16[544,256]{1,0:T(8,128)(2,1)S(1)}, u32[]{:S(2)}, u32[]{:S(2)}) collective-permute-start(bf16[544,256]{1,0:T(8,128)(2,1)S(1)} %collective-permute-done.3.refs_2_), channel_id=1, source_target_pairs={{0,192},{16,208},{32,224},{48,240},{64,0},{80,16},{96,32},{112,48}... | collective-permute-start | bytes 835592 | tf_op jit(solution)/shard_map/ppermute | solution.py:152
  103.0 14.1 %collective-permute-start.25 = (bf16[544,256]{1,0:T(8,128)(2,1)S(1)}, bf16[544,256]{1,0:T(8,128)(2,1)S(1)}, u32[]{:S(2)}, u32[]{:S(2)}) collective-permute-start(bf16[544,256]{1,0:T(8,128)(2,1)S(1)} %collective-permute-done.17.refs_2_.refs_9_), channel_id=1, source_target_pairs={{0,16},{16,32},{32,48},{48,0},{64,80},{80,96},{96,112},{112,64},{1... | collective-permute-start | bytes 835592 | tf_op jit(solution)/shard_map/ppermute | solution.py:152
  109.3 22.3 %collective-permute-start.13 = (bf16[1080,256]{1,0:T(8,128)(2,1)S(1)}, bf16[1080,256]{1,0:T(8,128)(2,1)S(1)}, u32[]{:S(2)}, u32[]{:S(2)}) collective-permute-start(bf16[1080,256]{1,0:T(8,128)(2,1)S(1)} %collective-permute-done.12.refs_4_), channel_id=1, source_target_pairs={{0,192},{16,208},{32,224},{48,240},{64,0},{80,16},{96,32},{112,48}... | collective-permute-start | bytes 1658888 | tf_op jit(solution)/shard_map/ppermute | solution.py:152
  116.7 16.0 %collective-permute-start.35 = (bf16[1080,256]{1,0:T(8,128)(2,1)S(1)}, bf16[1080,256]{1,0:T(8,128)(2,1)S(1)}, u32[]{:S(2)}, u32[]{:S(2)}) collective-permute-start(bf16[1080,256]{1,0:T(8,128)(2,1)S(1)} %collective-permute-done.34.refs_4_.refs_5_), channel_id=1, source_target_pairs={{0,48},{16,0},{32,16},{48,32},{64,112},{80,64},{96,80},{112,96},{1... | collective-permute-start | bytes 1658888 | tf_op jit(solution)/shard_map/ppermute | solution.py:152
  117.1 27.8 %collective-permute-start.2 = (bf16[1080,256]{1,0:T(8,128)(2,1)S(1)}, bf16[1080,256]{1,0:T(8,128)(2,1)S(1)}, u32[]{:S(2)}, u32[]{:S(2)}) collective-permute-start(bf16[1080,256]{1,0:T(8,128)(2,1)S(1)} %collective-permute-done.1.refs_1_), channel_id=1, source_target_pairs={{0,64},{16,80},{32,96},{48,112},{64,128},{80,144},{96,160},{112,17... | collective-permute-start | bytes 1658888 | tf_op jit(solution)/shard_map/ppermute | solution.py:152
  123.1 21.7 %collective-permute-start.16 = (bf16[1080,256]{1,0:T(8,128)(2,1)S(1)}, bf16[1080,256]{1,0:T(8,128)(2,1)S(1)}, u32[]{:S(2)}, u32[]{:S(2)}) collective-permute-start(bf16[1080,256]{1,0:T(8,128)(2,1)S(1)} %collective-permute-done.15.refs_1_.refs_8_), channel_id=1, source_target_pairs={{0,16},{16,32},{32,48},{48,0},{64,80},{80,96},{96,112},{112,64},{1... | collective-permute-start | bytes 1658888 | tf_op jit(solution)/shard_map/ppermute | solution.py:152
  127.9 16.9 %collective-permute-start.5 = (bf16[544,256]{1,0:T(8,128)(2,1)S(1)}, bf16[544,256]{1,0:T(8,128)(2,1)S(1)}, u32[]{:S(2)}, u32[]{:S(2)}) collective-permute-start(bf16[544,256]{1,0:T(8,128)(2,1)S(1)} %collective-permute-done.4.refs_2_), channel_id=1, source_target_pairs={{0,192},{16,208},{32,224},{48,240},{64,0},{80,16},{96,32},{112,48}... | collective-permute-start | bytes 835592 | tf_op jit(solution)/shard_map/ppermute | solution.py:152
  131.6 13.3 %collective-permute-start.19 = (bf16[544,256]{1,0:T(8,128)(2,1)S(1)}, bf16[544,256]{1,0:T(8,128)(2,1)S(1)}, u32[]{:S(2)}, u32[]{:S(2)}) collective-permute-start(bf16[544,256]{1,0:T(8,128)(2,1)S(1)} %collective-permute-done.18.refs_2_.refs_12_), channel_id=1, source_target_pairs={{0,48},{16,0},{32,16},{48,32},{64,112},{80,64},{96,80},{112,96},{1... | collective-permute-start | bytes 835592 | tf_op jit(solution)/shard_map/ppermute | solution.py:152
  132.8 12.1 %collective-permute-start.23 = (bf16[536,256]{1,0:T(8,128)(2,1)S(1)}, bf16[536,256]{1,0:T(8,128)(2,1)S(1)}, u32[]{:S(2)}, u32[]{:S(2)}) collective-permute-start(bf16[536,256]{1,0:T(8,128)(2,1)S(1)} %collective-permute-done.22.refs_3_.refs_13_), channel_id=1, source_target_pairs={{0,48},{16,0},{32,16},{48,32},{64,112},{80,64},{96,80},{112,96},{1... | collective-permute-start | bytes 823304 | tf_op jit(solution)/shard_map/ppermute | solution.py:152
  (8 other events, 63.5 us)

commit v2 on v1

--- a/solution.py
+++ b/solution.py
@@ -18,20 +18,20 @@
 HALF = 64
 QUART = COLS // 4
 PIECE = COLS + QUART
-CUT = 544
+CUT = 624
 SIDE = 4
 
 
-def pack_kernel(w_ref, f_ref, o_ref):
+def pack_kernel(m, w_ref, tops_ref, o_ref):
     odd = lax.axis_index("zero") % 2
     full_at = pl.multiple_of(odd * HALF, 8)
     half_at = pl.multiple_of((1 - odd) * FULL, 8)
+    factor = jnp.max(tops_ref[:, m, :], axis=0, keepdims=True)
     for at in range(0, COLS, 128):
         n = min(128, COLS - at)
-        f = f_ref[:, at : at + n]
-        w = w_ref[pl.ds(full_at, FULL), at : at + n] / f
+        w = w_ref[pl.ds(full_at, FULL), at : at + n] / factor[:, at : at + n]
         o_ref[at : at + n, :] = w.T.astype(jnp.bfloat16)
-    h = w_ref[pl.ds(half_at, HALF), :] / f_ref[...]
+    h = w_ref[pl.ds(half_at, HALF), :] / factor
     t = jnp.concatenate([h, h], axis=0).T
     low = lax.broadcasted_iota(jnp.int32, (2 * QUART, 128), 1) < HALF
     keep = jnp.logical_xor(low, odd == 1)
@@ -40,15 +40,15 @@
     o_ref[COLS:, 128:] = p[QUART:]
 
 
-def packed(w, f):
+def packed(w, tops, m):
     return pl.pallas_call(
-        pack_kernel,
+        functools.partial(pack_kernel, m),
         out_shape=jax.ShapeDtypeStruct((PIECE, 256), jnp.bfloat16),
         in_specs=[pl.BlockSpec(memory_space=pltpu.VMEM)] * 2,
         out_specs=pl.BlockSpec(memory_space=pltpu.VMEM),
         compiler_params=pltpu.CompilerParams(vmem_limit_bytes=8 << 20),
         cost_estimate=pl.CostEstimate(flops=4_000_000, bytes_accessed=1_600_000, transcendentals=0),
-    )(w, f.reshape(1, COLS))
+    )(w, tops)
 
 
 def tile_of(kx, ky):
@@ -71,9 +71,9 @@
     odd = lax.axis_index("zero") % 2
     done = []
     for (layout, fulls, _), out in zip(plan, outs):
-        for key in fulls:
+        for key, part in fulls:
             at = tile_of(*key)
-            for r, a, b in layout[key]:
+            for r, a, b in [layout[key, q] for q in part]:
                 hi = min(b, COLS)
                 if hi > a:
                     c = pltpu.make_async_copy(
@@ -87,7 +87,7 @@
     for (layout, _, pairs), out in zip(plan, outs):
 
         def half(key, lanes):
-            r, a, _ = layout[key][-1]
+            r, a, _ = layout[key, -1]
             return ins[r][COLS - a : PIECE - a, lanes].astype(jnp.float32)
 
         for p, ky in pairs:
@@ -116,18 +116,21 @@
     refs, plan = [], []
     for _, got, fulls, pairs in jobs:
         layout = {}
-        for key in list(fulls) + [(k, ky) for p, ky in pairs for k in (2 * p, 1, 3)]:
-            if key not in layout:
-                layout[key], at = [], 0
-                for part in got[key]:
-                    layout[key].append((len(refs), at, at + part.shape[0]))
-                    refs.append(part)
-                    at += part.shape[0]
+        need = [(key, q) for key, part in fulls for q in part]
+        need += [((k, ky), -1) for p, ky in pairs for k in (2 * p, 1, 3)]
+        for key, q in need:
+            parts = got[key]
+            one = parts[q]
+            if not any(one is r for r in refs):
+                refs.append(one)
+            r = [one is x for x in refs].index(True)
+            at = sum(x.shape[0] for x in parts[: q % len(parts)])
+            layout[key, q] = (r, at, at + one.shape[0])
         plan.append((layout, tuple(fulls), tuple(pairs)))
     first = jobs[0][0] is None
     olds = [] if first else [j[0] for j in jobs]
     n_tiles = max(1, sum(len(j[3]) for j in jobs))
-    n_full = max(1, sum(len(layout[k]) for layout, fulls, _ in plan for k in fulls))
+    n_full = max(1, sum(len(part) for _, fulls, _ in plan for _, part in fulls))
     shape = jax.ShapeDtypeStruct((COLS, ROWS * SIDE * SIDE), jnp.bfloat16)
     return pl.pallas_call(
         functools.partial(place_kernel, plan, len(refs), first),
@@ -140,7 +143,7 @@
             pltpu.SemaphoreType.DMA((n_tiles,)),
         ],
         input_output_aliases={len(refs) + i: i for i in range(len(olds))},
-        compiler_params=pltpu.CompilerParams(vmem_limit_bytes=16 << 20),
+        compiler_params=pltpu.CompilerParams(vmem_limit_bytes=6 << 20),
         cost_estimate=pl.CostEstimate(flops=1_000_000, bytes_accessed=4_000_000, transcendentals=0),
     )(*refs, *olds)
 
@@ -153,21 +156,21 @@
 
 
 ORDER = [
-    *"gs+0 gs-0 us+0 us-0".split(),
+    *"gs+0 us+0 gs-0 us-0".split(),
     *"ub+0 gb+0 ub-0 gb-0".split(),
-    *"gt+1 gt-3 ut+1 ut-3".split(),
-    *"ub+1 ub-3 gb+1 gb-3".split(),
+    *"gt+1 ut+1 gt-3 ut-3".split(),
+    *"ub+1 gb+1 ub-3 gb-3".split(),
     *"ub+3 gb+3".split(),
     *"ub-2a gb-2a ub-2b gb-2b".split(),
     *"ub+2a gb+2a ub+2b gb+2b".split(),
     *"ub-1 gb-1".split(),
     *"Pg0 Pu0".split(),
     *"uf+0 gf+0 uf-3 gf-3".split(),
-    *"uf+1 gf+1 uf-2a gf-2a".split(),
-    *"uf-2b gf-2b".split(),
+    *"uf+1a gf+1a uf-2a gf-2a".split(),
+    *"uf+1b gf+1b uf-2b gf-2b".split(),
     *"Pg1 Pu1 Pg3 Pu3".split(),
     *"Pg2 Pu2".split(),
-    *"Pend".split(),
+    *"Pmid Pend".split(),
 ]
 
 
@@ -181,16 +184,25 @@
         return shift(a, d, 0) if on_x else shift(a, 0, d)
 
     def pieces(m):
-        parts = lambda get: {k: [get(q) for q in ("2a", "2b")] if k == 2 else [get(str(k))] for k in range(SIDE)}
         got = {}
         for step in range(SIDE):
-            from_step = (lambda q: small[m][q]) if step == 0 else (lambda q: large[m].get((step, q)))
-            for k, v in parts(from_step).items():
-                got[(k, step) if m == "g" else (step, k)] = v
+            have = small[m] if step == 0 else {q: v for (s, q), v in large[m].items() if s == step}
+            for k in range(SIDE):
+                names = [str(k)] if str(k) in have else [f"{k}a", f"{k}b"]
+                got[(k, step) if m == "g" else (step, k)] = [have.get(q) for q in names]
         return got
 
-    def put(*jobs):
-        res = place([(out[m], pieces(m), fulls, pairs) for m, fulls, pairs in jobs])
+    def whole(m, keys):
+        return [(key, tuple(range(len(pieces(m)[key])) if (pieces(m)[key][0] is not None) else ())) for key in keys]
+
+    def put(name, *jobs):
+        split = {"Pmid": (0,), "Pend": (1,)}
+        res = place(
+            [
+                (out[m], pieces(m), [(k, split[name]) if name in split else w for k, w in zip(keys, whole(m, keys))], pairs)
+                for m, keys, pairs in jobs
+            ],
+        )
         for (m, _, _), r in zip(jobs, res):
             out[m] = r
 
@@ -204,6 +216,7 @@
         "Pu1": [("u", [(1, k) for k in every], [])],
         "Pu3": [("u", [(3, k) for k in every], [(0, k) for k in every])],
         "Pu2": [("u", [(2, 0), (2, 3)], [(1, 0), (1, 3)])],
+        "Pmid": [("g", [(1, 2), (2, 2)], []), ("u", [(2, 1), (2, 2)], [])],
         "Pend": [
             ("g", [(1, 2), (2, 2)], [(0, 2), (1, 2)]),
             ("u", [(2, 1), (2, 2)], [(1, 1), (1, 2)]),
@@ -211,7 +224,7 @@
     }
     for name in ORDER:
         if name[0] == "P":
-            put(*kernels[name])
+            put(name, *kernels[name])
             continue
         m, kind, sign, q = name[0], name[1], name[2], name[3:]
         on_x = (m == "g") == (kind in "st")
@@ -223,14 +236,13 @@
             small[m]["2a" if sign == "+" else "2b"] = move(part, on_x, sign)
         elif kind == "b":
             large[m][(step, q)] = move(small[m][q], on_x, sign)
+        elif q == "1a":
+            large[m][(2, q)] = move(large[m][(step, "1")][:CUT], on_x, sign)
+        elif q == "1b":
+            large[m][(2, q)] = move(large[m][(step, "1")][CUT:], on_x, sign)
         else:
             large[m][(2, q)] = move(large[m][(step, q)], on_x, sign)
     return out["g"], out["u"]
-
-
-def sent_to_all(array, axis):
-    count = lax.axis_size(axis)
-    return lax.all_to_all(jnp.broadcast_to(array[None], (count, *array.shape)), axis, 0, 0, tiled=True)
 
 
 def body(train_gate, drift_gate, spread_gate, train_up, drift_up, spread_up, norm_gain):
@@ -240,14 +252,13 @@
     whole_up = train_up - learn_rate * hold_up
     gained_gate = whole_gate * norm_gain[:, None]
     gained_up = whole_up * norm_gain[:, None]
-    tops = jnp.concatenate([jnp.max(jnp.abs(gained_gate), axis=0), jnp.max(jnp.abs(gained_up), axis=0)])
-    tops = sent_to_all(tops, "zero").max(axis=0)
-    factor_gate, factor_up = tops[:COLS], tops[COLS:]
-
-    gate = packed(gained_gate, factor_gate)
-    up = packed(gained_up, factor_up)
+    tops = jnp.stack([jnp.max(jnp.abs(gained_gate), axis=0), jnp.max(jnp.abs(gained_up), axis=0)])
+    tops = lax.all_to_all(jnp.broadcast_to(tops, (SIDE * SIDE, 2, COLS)), "zero", 0, 0, tiled=True)
+    gate = packed(gained_gate, tops, 0)
+    up = packed(gained_up, tops, 1)
+    factor_gate, factor_up = tops[:, 0].max(axis=0), tops[:, 1].max(axis=0)
     serving_gate, serving_up = spread(gate, up)
-    return serving_gate.T, serving_up.T, factor_gate, factor_up
+    return serving_gate.T, serving_up.T, factor_gate.reshape(COLS), factor_up.reshape(COLS)
 
 
 def solution(mesh):

time: 147 us -> 151 us (1.027)
  the two profiles are of different devices: /device:TPU:128 before, /device:TPU:30 now
where the time goes in v2:
time: 151 us
  waiting for transfers between devices  73.9 us (49%)
  starting transfers between devices  47.1 us (31%)
  Pallas kernels  13.5 us (9%)
  blocking collectives  11.1 us (7%)
  other arithmetic  4.2 us (3%)
    ppermute x40, waiting for transfers between devices, shift(): return lax.ppermute(a, 'zero', pairs)  73.9 us
    ppermute x40, starting transfers between devices, shift(): return lax.ppermute(a, 'zero', pairs)  47.1 us
    pallas_call x10, Pallas kernels, place(): pl.pallas_call(functools.partial(place_kernel, plan, len(refs), first), o...  13 us
    all_to_all x1, blocking collectives, body(): lax.all_to_all(jnp.broadcast_to(tops, (SIDE * SIDE, 2, COLS)), 'zero', 0,...  11.1 us
    reduce_max x1, other arithmetic, body(): jnp.max(jnp.abs(gained_up), axis=0)  3.49 us
  transfers between devices with their start and end apart: 40, of which 17 were waited for; matrix products, arithmetic and copies ran while one was open for 1% of the time, Pallas kernels for 8%

profile of v2, /device:TPU:30, one launch (start us, length us, event | category | flops | bytes accessed | tf_op | source)
XLA Modules:
  0.0 151.1 jit_solution(10063398896415017610)
XLA Ops:
  0.6 3.5 %abs_reduce_fusion = (f32[864]{0:T(1024)S(1)}, f32[320,864]{1,0:T(8,128)S(1)}, f32[864]{0:T(1024)S(1)}, f32[320,864]{1,0:T(8,128)S(1)}) fusion(f32[320]{0:T(512)} %param.13, f32[320,864]{1,0:T(8,128)} %param.10, f32[320,864]{1,0:T(8,128)} %param.12, f32[320,864]{1,0:T(8,128)} %param.11, f32[320,864]{1,0:T(8,128)} %param.7, f32[320,864]{1,0:T(8,128)} %param.9, ...), kind=kLoop, calls=%fused_computation | loop fusion | flops 3868992 | bytes 8855552 | tf_op jit(solution)/shard_map/reduce_max | solution.py:255
  4.2 11.1 %all_to_all.5.tops_ref = f32[16,2,864]{2,1,0:T(2,128)S(1)} all-to-all(f32[16,2,864]{2,1,0:T(2,128)S(1)} %broadcast_in_dim.2), channel_id=1, replica_groups=mesh['zero'=16,'width'=16] {'zero'}, dimensions={0} | all-to-all | bytes 221184 | tf_op jit(solution)/shard_map/all_to_all | solution.py:256
  16.3 2.6 %collective-permute-start.11 = (bf16[1080,256]{1,0:T(8,128)(2,1)S(1)}, bf16[1080,256]{1,0:T(8,128)(2,1)S(1)}, u32[]{:S(2)}, u32[]{:S(2)}) collective-permute-start(bf16[1080,256]{1,0:T(8,128)(2,1)S(1)} %shard_map.103.refs_0_.refs_5_), channel_id=1, source_target_pairs={{0,64},{16,80},{32,96},{48,112},{64,128},{80,144},{96,160},{112,17... | collective-permute-start | bytes 1658888 | tf_op jit(solution)/shard_map/ppermute | solution.py:155
  18.9 2.0 %collective-permute-start.33 = (bf16[1080,256]{1,0:T(8,128)(2,1)S(1)}, bf16[1080,256]{1,0:T(8,128)(2,1)S(1)}, u32[]{:S(2)}, u32[]{:S(2)}) collective-permute-start(bf16[1080,256]{1,0:T(8,128)(2,1)S(1)} %shard_map.103.refs_0_.refs_5_), channel_id=1, source_target_pairs={{0,16},{16,32},{32,48},{48,0},{64,80},{80,96},{96,112},{112,64},{1... | collective-permute-start | bytes 1658888 | tf_op jit(solution)/shard_map/ppermute | solution.py:155
  22.1 7.6 %collective-permute-done.14.refs_4_.refs_11_ = bf16[1080,256]{1,0:T(8,128)(2,1)S(1)} collective-permute-done((bf16[1080,256]{1,0:T(8,128)(2,1)S(1)}, bf16[1080,256]{1,0:T(8,128)(2,1)S(1)}, u32[]{:S(2)}, u32[]{:S(2)}) %collective-permute-start.14) | collective-permute-done | bytes 552992 | tf_op jit(solution)/shard_map/ppermute | solution.py:155
  29.8 2.0 %collective-permute-start = (bf16[1080,256]{1,0:T(8,128)(2,1)S(1)}, bf16[1080,256]{1,0:T(8,128)(2,1)S(1)}, u32[]{:S(2)}, u32[]{:S(2)}) collective-permute-start(bf16[1080,256]{1,0:T(8,128)(2,1)S(1)} %shard_map.102.refs_0_), channel_id=1, source_target_pairs={{0,16},{16,32},{32,48},{48,0},{64,80},{80,96},{96,112},{112,64},{1... | collective-permute-start | bytes 1658888 | tf_op jit(solution)/shard_map/ppermute | solution.py:155
  33.8 3.7 %collective-permute-done.37.refs_0_.refs_3_ = bf16[1080,256]{1,0:T(8,128)(2,1)S(1)} collective-permute-done((bf16[1080,256]{1,0:T(8,128)(2,1)S(1)}, bf16[1080,256]{1,0:T(8,128)(2,1)S(1)}, u32[]{:S(2)}, u32[]{:S(2)}) %collective-permute-start.37) | collective-permute-done | bytes 552992 | tf_op jit(solution)/shard_map/ppermute | solution.py:155
  37.6 8.4 %collective-permute-done.3.refs_4_ = bf16[1080,256]{1,0:T(8,128)(2,1)S(1)} collective-permute-done((bf16[1080,256]{1,0:T(8,128)(2,1)S(1)}, bf16[1080,256]{1,0:T(8,128)(2,1)S(1)}, u32[]{:S(2)}, u32[]{:S(2)}) %collective-permute-start.3) | collective-permute-done | bytes 552992 | tf_op jit(solution)/shard_map/ppermute | solution.py:155
  47.3 3.3 %collective-permute-start.21 = (bf16[624,256]{1,0:T(8,128)(2,1)S(1)}, bf16[624,256]{1,0:T(8,128)(2,1)S(1)}, u32[]{:S(2)}, u32[]{:S(2)}) collective-permute-start(bf16[624,256]{1,0:T(8,128)(2,1)S(1)} %slice.45), channel_id=1, source_target_pairs={{0,16},{16,32},{32,48},{48,0},{64,80},{80,96},{96,112},{112,64},{1... | collective-permute-start | bytes 958472 | tf_op jit(solution)/shard_map/ppermute | solution.py:155
  50.6 1.8 %collective-permute-start.19 = (bf16[456,256]{1,0:T(8,128)(2,1)S(1)}, bf16[456,256]{1,0:T(8,128)(2,1)S(1)}, u32[]{:S(2)}, u32[]{:S(2)}) collective-permute-start(bf16[456,256]{1,0:T(8,128)(2,1)S(1)} %collective-permute-done.15.refs_3_.refs_9_), channel_id=1, source_target_pairs={{0,16},{16,32},{32,48},{48,0},{64,80},{80,96},{96,112},{112,64},{1... | collective-permute-start | bytes 700424 | tf_op jit(solution)/shard_map/ppermute | solution.py:155
  52.6 3.4 %collective-permute-done.4.refs_3_ = bf16[456,256]{1,0:T(8,128)(2,1)S(1)} collective-permute-done((bf16[456,256]{1,0:T(8,128)(2,1)S(1)}, bf16[456,256]{1,0:T(8,128)(2,1)S(1)}, u32[]{:S(2)}, u32[]{:S(2)}) %collective-permute-start.4) | collective-permute-done | bytes 233504 | tf_op jit(solution)/shard_map/ppermute | solution.py:155
  56.1 2.5 %collective-permute-done.21.refs_2_ = bf16[624,256]{1,0:T(8,128)(2,1)S(1)} collective-permute-done((bf16[624,256]{1,0:T(8,128)(2,1)S(1)}, bf16[624,256]{1,0:T(8,128)(2,1)S(1)}, u32[]{:S(2)}, u32[]{:S(2)}) %collective-permute-start.21) | collective-permute-done | bytes 319520 | tf_op jit(solution)/shard_map/ppermute | solution.py:155
  59.4 4.1 %collective-permute-done.19.refs_3_.refs_10_.refs_8_ = bf16[456,256]{1,0:T(8,128)(2,1)S(1)} collective-permute-done((bf16[456,256]{1,0:T(8,128)(2,1)S(1)}, bf16[456,256]{1,0:T(8,128)(2,1)S(1)}, u32[]{:S(2)}, u32[]{:S(2)}) %collective-permute-start.19) | collective-permute-done | bytes 233504 | tf_op jit(solution)/shard_map/ppermute | solution.py:155
  63.5 3.7 %collective-permute-start.38 = (bf16[1080,256]{1,0:T(8,128)(2,1)S(1)}, bf16[1080,256]{1,0:T(8,128)(2,1)S(1)}, u32[]{:S(2)}, u32[]{:S(2)}) collective-permute-start(bf16[1080,256]{1,0:T(8,128)(2,1)S(1)} %collective-permute-done.14.refs_4_.refs_11_), channel_id=1, source_target_pairs={{0,16},{16,32},{32,48},{48,0},{64,80},{80,96},{96,112},{112,64},{1... | collective-permute-start | bytes 1658888 | tf_op jit(solution)/shard_map/ppermute | solution.py:155
  67.3 3.2 %collective-permute-start.34 = (bf16[1080,256]{1,0:T(8,128)(2,1)S(1)}, bf16[1080,256]{1,0:T(8,128)(2,1)S(1)}, u32[]{:S(2)}, u32[]{:S(2)}) collective-permute-start(bf16[1080,256]{1,0:T(8,128)(2,1)S(1)} %collective-permute-done.33.refs_0_.refs_6_.refs_2_), channel_id=1, source_target_pairs={{0,16},{16,32},{32,48},{48,0},{64,80},{80,96},{96,112},{112,64},{1... | collective-permute-start | bytes 1658888 | tf_op jit(solution)/shard_map/ppermute | solution.py:155
  70.6 4.8 %collective-permute-done.12.refs_1_.refs_8_.refs_6_ = bf16[1080,256]{1,0:T(8,128)(2,1)S(1)} collective-permute-done((bf16[1080,256]{1,0:T(8,128)(2,1)S(1)}, bf16[1080,256]{1,0:T(8,128)(2,1)S(1)}, u32[]{:S(2)}, u32[]{:S(2)}) %collective-permute-start.12) | collective-permute-done | bytes 552992 | tf_op jit(solution)/shard_map/ppermute | solution.py:155
  75.7 11.6 %collective-permute-done.38.refs_4_.refs_12_ = bf16[1080,256]{1,0:T(8,128)(2,1)S(1)} collective-permute-done((bf16[1080,256]{1,0:T(8,128)(2,1)S(1)}, bf16[1080,256]{1,0:T(8,128)(2,1)S(1)}, u32[]{:S(2)}, u32[]{:S(2)}) %collective-permute-start.38) | collective-permute-done | bytes 552992 | tf_op jit(solution)/shard_map/ppermute | solution.py:155
  87.5 1.7 %collective-permute-start.9 = (bf16[1080,256]{1,0:T(8,128)(2,1)S(1)}, bf16[1080,256]{1,0:T(8,128)(2,1)S(1)}, u32[]{:S(2)}, u32[]{:S(2)}) collective-permute-start(bf16[1080,256]{1,0:T(8,128)(2,1)S(1)} %collective-permute-done.3.refs_4_), channel_id=1, source_target_pairs={{0,192},{16,208},{32,224},{48,240},{64,0},{80,16},{96,32},{112,48}... | collective-permute-start | bytes 1658888 | tf_op jit(solution)/shard_map/ppermute | solution.py:155
  90.2 5.3 %collective-permute-done.34.refs_0_ = bf16[1080,256]{1,0:T(8,128)(2,1)S(1)} collective-permute-done((bf16[1080,256]{1,0:T(8,128)(2,1)S(1)}, bf16[1080,256]{1,0:T(8,128)(2,1)S(1)}, u32[]{:S(2)}, u32[]{:S(2)}) %collective-permute-start.34) | collective-permute-done | bytes 552992 | tf_op jit(solution)/shard_map/ppermute | solution.py:155
  95.5 3.4 %collective-permute-start.39 = (bf16[624,256]{1,0:T(8,128)(2,1)S(1)}, bf16[624,256]{1,0:T(8,128)(2,1)S(1)}, u32[]{:S(2)}, u32[]{:S(2)}) collective-permute-start(bf16[624,256]{1,0:T(8,128)(2,1)S(1)} %collective-permute-done.25.refs_2_), channel_id=1, source_target_pairs={{0,16},{16,32},{32,48},{48,0},{64,80},{80,96},{96,112},{112,64},{1... | collective-permute-start | bytes 958472 | tf_op jit(solution)/shard_map/ppermute | solution.py:155
  98.9 2.3 %collective-permute-done.32.refs_4_ = bf16[1080,256]{1,0:T(8,128)(2,1)S(1)} collective-permute-done((bf16[1080,256]{1,0:T(8,128)(2,1)S(1)}, bf16[1080,256]{1,0:T(8,128)(2,1)S(1)}, u32[]{:S(2)}, u32[]{:S(2)}) %collective-permute-start.32) | collective-permute-done | bytes 552992 | tf_op jit(solution)/shard_map/ppermute | solution.py:155
  101.2 1.5 collective-permute-start.30
  102.7 6.8 %collective-permute-done.29.refs_1_ = bf16[1080,256]{1,0:T(8,128)(2,1)S(1)} collective-permute-done((bf16[1080,256]{1,0:T(8,128)(2,1)S(1)}, bf16[1080,256]{1,0:T(8,128)(2,1)S(1)}, u32[]{:S(2)}, u32[]{:S(2)}) %collective-permute-start.29) | collective-permute-done | bytes 552992 | tf_op jit(solution)/shard_map/ppermute | solution.py:155
  109.5 1.5 collective-permute-start.22
  112.9 3.8 %collective-permute-start.24 = (bf16[624,256]{1,0:T(8,128)(2,1)S(1)}, bf16[624,256]{1,0:T(8,128)(2,1)S(1)}, u32[]{:S(2)}, u32[]{:S(2)}) collective-permute-start(bf16[624,256]{1,0:T(8,128)(2,1)S(1)} %slice.46), channel_id=1, source_target_pairs={{0,16},{16,32},{32,48},{48,0},{64,80},{80,96},{96,112},{112,64},{1... | collective-permute-start | bytes 958472 | tf_op jit(solution)/shard_map/ppermute | solution.py:155
  117.2 2.0 %collective-permute-start.20 = (bf16[624,256]{1,0:T(8,128)(2,1)S(1)}, bf16[624,256]{1,0:T(8,128)(2,1)S(1)}, u32[]{:S(2)}, u32[]{:S(2)}) collective-permute-start(bf16[624,256]{1,0:T(8,128)(2,1)S(1)} %slice.44), channel_id=1, source_target_pairs={{0,64},{16,80},{32,96},{48,112},{64,128},{80,144},{96,160},{112,17... | collective-permute-start | bytes 958472 | tf_op jit(solution)/shard_map/ppermute | solution.py:155
  121.4 2.8 %collective-permute-done.20.refs_0_ = bf16[624,256]{1,0:T(8,128)(2,1)S(1)} collective-permute-done((bf16[624,256]{1,0:T(8,128)(2,1)S(1)}, bf16[624,256]{1,0:T(8,128)(2,1)S(1)}, u32[]{:S(2)}, u32[]{:S(2)}) %collective-permute-start.20) | collective-permute-done | bytes 319520 | tf_op jit(solution)/shard_map/ppermute | solution.py:155
  124.2 7.9 %collective-permute-done.27.refs_3_ = bf16[624,256]{1,0:T(8,128)(2,1)S(1)} collective-permute-done((bf16[624,256]{1,0:T(8,128)(2,1)S(1)}, bf16[624,256]{1,0:T(8,128)(2,1)S(1)}, u32[]{:S(2)}, u32[]{:S(2)}) %collective-permute-start.27) | collective-permute-done | bytes 319520 | tf_op jit(solution)/shard_map/ppermute | solution.py:155
  132.6 1.7 %collective-permute-start.13 = (bf16[456,256]{1,0:T(8,128)(2,1)S(1)}, bf16[456,256]{1,0:T(8,128)(2,1)S(1)}, u32[]{:S(2)}, u32[]{:S(2)}) collective-permute-start(bf16[456,256]{1,0:T(8,128)(2,1)S(1)} %slice.42), channel_id=1, source_target_pairs={{0,16},{16,32},{32,48},{48,0},{64,80},{80,96},{96,112},{112,64},{1... | collective-permute-start | bytes 700424 | tf_op jit(solution)/shard_map/ppermute | solution.py:155
  134.4 2.7 %collective-permute-start.2 = (bf16[456,256]{1,0:T(8,128)(2,1)S(1)}, bf16[456,256]{1,0:T(8,128)(2,1)S(1)}, u32[]{:S(2)}, u32[]{:S(2)}) collective-permute-start(bf16[456,256]{1,0:T(8,128)(2,1)S(1)} %slice.40), channel_id=1, source_target_pairs={{0,64},{16,80},{32,96},{48,112},{64,128},{80,144},{96,160},{112,17... | collective-permute-start | bytes 700424 | tf_op jit(solution)/shard_map/ppermute | solution.py:155
  141.8 1.6 %shard_map.110.refs_6_ = bf16[864,5120]{1,0:T(8,128)(2,1)} custom-call(bf16[1080,256]{1,0:T(8,128)(2,1)S(1)} %collective-permute-done.37.refs_0_.refs_3_, bf16[1080,256]{1,0:T(8,128)(2,1)S(1)} %collective-permute-done.18.refs_1_.refs_7_, bf16[624,256]{1,0:T(8,128)(2,1)S(1)} %collective-permute-done.26.refs_2_, ...), custom_call_target="tpu_custom_call", output_to_operand_aliasing={{}: (13, {})} | custom-call | flops 1000000 | bytes 4000000 | tf_op jit(solution)/shard_map/pallas_call | solution.py:135
  143.4 1.4 shard_map.105.refs_5_
  (75 shorter events, 24.2 us)
Async XLA Ops:
  15.6 14.1 %collective-permute-start.14 = (bf16[1080,256]{1,0:T(8,128)(2,1)S(1)}, bf16[1080,256]{1,0:T(8,128)(2,1)S(1)}, u32[]{:S(2)}, u32[]{:S(2)}) collective-permute-start(bf16[1080,256]{1,0:T(8,128)(2,1)S(1)} %shard_map.103.refs_0_.refs_5_), channel_id=1, source_target_pairs={{0,192},{16,208},{32,224},{48,240},{64,0},{80,16},{96,32},{112,48}... | collective-permute-start | bytes 1658888 | tf_op jit(solution)/shard_map/ppermute | solution.py:155
  16.3 15.4 %collective-permute-start.11 = (bf16[1080,256]{1,0:T(8,128)(2,1)S(1)}, bf16[1080,256]{1,0:T(8,128)(2,1)S(1)}, u32[]{:S(2)}, u32[]{:S(2)}) collective-permute-start(bf16[1080,256]{1,0:T(8,128)(2,1)S(1)} %shard_map.103.refs_0_.refs_5_), channel_id=1, source_target_pairs={{0,64},{16,80},{32,96},{48,112},{64,128},{80,144},{96,160},{112,17... | collective-permute-start | bytes 1658888 | tf_op jit(solution)/shard_map/ppermute | solution.py:155
  18.9 14.0 %collective-permute-start.33 = (bf16[1080,256]{1,0:T(8,128)(2,1)S(1)}, bf16[1080,256]{1,0:T(8,128)(2,1)S(1)}, u32[]{:S(2)}, u32[]{:S(2)}) collective-permute-start(bf16[1080,256]{1,0:T(8,128)(2,1)S(1)} %shard_map.103.refs_0_.refs_5_), channel_id=1, source_target_pairs={{0,16},{16,32},{32,48},{48,0},{64,80},{80,96},{96,112},{112,64},{1... | collective-permute-start | bytes 1658888 | tf_op jit(solution)/shard_map/ppermute | solution.py:155
  20.9 16.6 %collective-permute-start.37 = (bf16[1080,256]{1,0:T(8,128)(2,1)S(1)}, bf16[1080,256]{1,0:T(8,128)(2,1)S(1)}, u32[]{:S(2)}, u32[]{:S(2)}) collective-permute-start(bf16[1080,256]{1,0:T(8,128)(2,1)S(1)} %shard_map.103.refs_0_.refs_5_), channel_id=1, source_target_pairs={{0,48},{16,0},{32,16},{48,32},{64,112},{80,64},{96,80},{112,96},{1... | collective-permute-start | bytes 1658888 | tf_op jit(solution)/shard_map/ppermute | solution.py:155
  21.2 24.8 %collective-permute-start.3 = (bf16[1080,256]{1,0:T(8,128)(2,1)S(1)}, bf16[1080,256]{1,0:T(8,128)(2,1)S(1)}, u32[]{:S(2)}, u32[]{:S(2)}) collective-permute-start(bf16[1080,256]{1,0:T(8,128)(2,1)S(1)} %shard_map.102.refs_0_), channel_id=1, source_target_pairs={{0,48},{16,0},{32,16},{48,32},{64,112},{80,64},{96,80},{112,96},{1... | collective-permute-start | bytes 1658888 | tf_op jit(solution)/shard_map/ppermute | solution.py:155
  29.8 17.4 %collective-permute-start = (bf16[1080,256]{1,0:T(8,128)(2,1)S(1)}, bf16[1080,256]{1,0:T(8,128)(2,1)S(1)}, u32[]{:S(2)}, u32[]{:S(2)}) collective-permute-start(bf16[1080,256]{1,0:T(8,128)(2,1)S(1)} %shard_map.102.refs_0_), channel_id=1, source_target_pairs={{0,16},{16,32},{32,48},{48,0},{64,80},{80,96},{96,112},{112,64},{1... | collective-permute-start | bytes 1658888 | tf_op jit(solution)/shard_map/ppermute | solution.py:155
  31.8 15.5 %collective-permute-start.7 = (bf16[1080,256]{1,0:T(8,128)(2,1)S(1)}, bf16[1080,256]{1,0:T(8,128)(2,1)S(1)}, u32[]{:S(2)}, u32[]{:S(2)}) collective-permute-start(bf16[1080,256]{1,0:T(8,128)(2,1)S(1)} %shard_map.102.refs_0_), channel_id=1, source_target_pairs={{0,64},{16,80},{32,96},{48,112},{64,128},{80,144},{96,160},{112,17... | collective-permute-start | bytes 1658888 | tf_op jit(solution)/shard_map/ppermute | solution.py:155
  32.9 19.5 %collective-permute-start.28 = (bf16[1080,256]{1,0:T(8,128)(2,1)S(1)}, bf16[1080,256]{1,0:T(8,128)(2,1)S(1)}, u32[]{:S(2)}, u32[]{:S(2)}) collective-permute-start(bf16[1080,256]{1,0:T(8,128)(2,1)S(1)} %shard_map.102.refs_0_), channel_id=1, source_target_pairs={{0,192},{16,208},{32,224},{48,240},{64,0},{80,16},{96,32},{112,48}... | collective-permute-start | bytes 1658888 | tf_op jit(solution)/shard_map/ppermute | solution.py:155
  37.6 13.1 %collective-permute-start.15 = (bf16[456,256]{1,0:T(8,128)(2,1)S(1)}, bf16[456,256]{1,0:T(8,128)(2,1)S(1)}, u32[]{:S(2)}, u32[]{:S(2)}) collective-permute-start(bf16[456,256]{1,0:T(8,128)(2,1)S(1)} %slice.43), channel_id=1, source_target_pairs={{0,192},{16,208},{32,224},{48,240},{64,0},{80,16},{96,32},{112,48}... | collective-permute-start | bytes 700424 | tf_op jit(solution)/shard_map/ppermute | solution.py:155
  50.6 12.9 %collective-permute-start.19 = (bf16[456,256]{1,0:T(8,128)(2,1)S(1)}, bf16[456,256]{1,0:T(8,128)(2,1)S(1)}, u32[]{:S(2)}, u32[]{:S(2)}) collective-permute-start(bf16[456,256]{1,0:T(8,128)(2,1)S(1)} %collective-permute-done.15.refs_3_.refs_9_), channel_id=1, source_target_pairs={{0,16},{16,32},{32,48},{48,0},{64,80},{80,96},{96,112},{112,64},{1... | collective-permute-start | bytes 700424 | tf_op jit(solution)/shard_map/ppermute | solution.py:155
  52.4 14.8 %collective-permute-start.16 = (bf16[456,256]{1,0:T(8,128)(2,1)S(1)}, bf16[456,256]{1,0:T(8,128)(2,1)S(1)}, u32[]{:S(2)}, u32[]{:S(2)}) collective-permute-start(bf16[456,256]{1,0:T(8,128)(2,1)S(1)} %collective-permute-done.15.refs_3_.refs_9_), channel_id=1, source_target_pairs={{0,48},{16,0},{32,16},{48,32},{64,112},{80,64},{96,80},{112,96},{1... | collective-permute-start | bytes 700424 | tf_op jit(solution)/shard_map/ppermute | solution.py:155
  56.1 19.3 %collective-permute-start.12 = (bf16[1080,256]{1,0:T(8,128)(2,1)S(1)}, bf16[1080,256]{1,0:T(8,128)(2,1)S(1)}, u32[]{:S(2)}, u32[]{:S(2)}) collective-permute-start(bf16[1080,256]{1,0:T(8,128)(2,1)S(1)} %collective-permute-done.11.refs_1_.refs_7_), channel_id=1, source_target_pairs={{0,16},{16,32},{32,48},{48,0},{64,80},{80,96},{96,112},{112,64},{1... | collective-permute-start | bytes 1658888 | tf_op jit(solution)/shard_map/ppermute | solution.py:155
  63.5 23.7 %collective-permute-start.38 = (bf16[1080,256]{1,0:T(8,128)(2,1)S(1)}, bf16[1080,256]{1,0:T(8,128)(2,1)S(1)}, u32[]{:S(2)}, u32[]{:S(2)}) collective-permute-start(bf16[1080,256]{1,0:T(8,128)(2,1)S(1)} %collective-permute-done.14.refs_4_.refs_11_), channel_id=1, source_target_pairs={{0,16},{16,32},{32,48},{48,0},{64,80},{80,96},{96,112},{112,64},{1... | collective-permute-start | bytes 1658888 | tf_op jit(solution)/shard_map/ppermute | solution.py:155
  67.2 20.3 %collective-permute-start.35 = (bf16[1080,256]{1,0:T(8,128)(2,1)S(1)}, bf16[1080,256]{1,0:T(8,128)(2,1)S(1)}, u32[]{:S(2)}, u32[]{:S(2)}) collective-permute-start(bf16[1080,256]{1,0:T(8,128)(2,1)S(1)} %collective-permute-done.14.refs_4_.refs_11_), channel_id=1, source_target_pairs={{0,48},{16,0},{32,16},{48,32},{64,112},{80,64},{96,80},{112,96},{1... | collective-permute-start | bytes 1658888 | tf_op jit(solution)/shard_map/ppermute | solution.py:155
  67.2 22.0 %collective-permute-start.18 = (bf16[1080,256]{1,0:T(8,128)(2,1)S(1)}, bf16[1080,256]{1,0:T(8,128)(2,1)S(1)}, u32[]{:S(2)}, u32[]{:S(2)}) collective-permute-start(bf16[1080,256]{1,0:T(8,128)(2,1)S(1)} %collective-permute-done.11.refs_1_.refs_7_), channel_id=1, source_target_pairs={{0,48},{16,0},{32,16},{48,32},{64,112},{80,64},{96,80},{112,96},{1... | collective-permute-start | bytes 1658888 | tf_op jit(solution)/shard_map/ppermute | solution.py:155
  67.3 28.1 %collective-permute-start.34 = (bf16[1080,256]{1,0:T(8,128)(2,1)S(1)}, bf16[1080,256]{1,0:T(8,128)(2,1)S(1)}, u32[]{:S(2)}, u32[]{:S(2)}) collective-permute-start(bf16[1080,256]{1,0:T(8,128)(2,1)S(1)} %collective-permute-done.33.refs_0_.refs_6_.refs_2_), channel_id=1, source_target_pairs={{0,16},{16,32},{32,48},{48,0},{64,80},{80,96},{96,112},{112,64},{1... | collective-permute-start | bytes 1658888 | tf_op jit(solution)/shard_map/ppermute | solution.py:155
  75.4 20.1 %collective-permute-start.1 = (bf16[1080,256]{1,0:T(8,128)(2,1)S(1)}, bf16[1080,256]{1,0:T(8,128)(2,1)S(1)}, u32[]{:S(2)}, u32[]{:S(2)}) collective-permute-start(bf16[1080,256]{1,0:T(8,128)(2,1)S(1)} %collective-permute-done.refs_1_), channel_id=1, source_target_pairs={{0,64},{16,80},{32,96},{48,112},{64,128},{80,144},{96,160},{112,17... | collective-permute-start | bytes 1658888 | tf_op jit(solution)/shard_map/ppermute | solution.py:155
  87.2 14.0 %collective-permute-start.32 = (bf16[1080,256]{1,0:T(8,128)(2,1)S(1)}, bf16[1080,256]{1,0:T(8,128)(2,1)S(1)}, u32[]{:S(2)}, u32[]{:S(2)}) collective-permute-start(bf16[1080,256]{1,0:T(8,128)(2,1)S(1)} %collective-permute-done.3.refs_4_), channel_id=1, source_target_pairs={{0,64},{16,80},{32,96},{48,112},{64,128},{80,144},{96,160},{112,17... | collective-permute-start | bytes 1658888 | tf_op jit(solution)/shard_map/ppermute | solution.py:155
  87.5 13.7 %collective-permute-start.9 = (bf16[1080,256]{1,0:T(8,128)(2,1)S(1)}, bf16[1080,256]{1,0:T(8,128)(2,1)S(1)}, u32[]{:S(2)}, u32[]{:S(2)}) collective-permute-start(bf16[1080,256]{1,0:T(8,128)(2,1)S(1)} %collective-permute-done.3.refs_4_), channel_id=1, source_target_pairs={{0,192},{16,208},{32,224},{48,240},{64,0},{80,16},{96,32},{112,48}... | collective-permute-start | bytes 1658888 | tf_op jit(solution)/shard_map/ppermute | solution.py:155
  89.3 20.2 %collective-permute-start.29 = (bf16[1080,256]{1,0:T(8,128)(2,1)S(1)}, bf16[1080,256]{1,0:T(8,128)(2,1)S(1)}, u32[]{:S(2)}, u32[]{:S(2)}) collective-permute-start(bf16[1080,256]{1,0:T(8,128)(2,1)S(1)} %collective-permute-done.refs_1_), channel_id=1, source_target_pairs={{0,192},{16,208},{32,224},{48,240},{64,0},{80,16},{96,32},{112,48}... | collective-permute-start | bytes 1658888 | tf_op jit(solution)/shard_map/ppermute | solution.py:155
  95.5 16.5 %collective-permute-start.8 = (bf16[1080,256]{1,0:T(8,128)(2,1)S(1)}, bf16[1080,256]{1,0:T(8,128)(2,1)S(1)}, u32[]{:S(2)}, u32[]{:S(2)}) collective-permute-start(bf16[1080,256]{1,0:T(8,128)(2,1)S(1)} %collective-permute-done.7.refs_0_), channel_id=1, source_target_pairs={{0,64},{16,80},{32,96},{48,112},{64,128},{80,144},{96,160},{112,17... | collective-permute-start | bytes 1658888 | tf_op jit(solution)/shard_map/ppermute | solution.py:155
  95.5 16.5 %collective-permute-start.39 = (bf16[624,256]{1,0:T(8,128)(2,1)S(1)}, bf16[624,256]{1,0:T(8,128)(2,1)S(1)}, u32[]{:S(2)}, u32[]{:S(2)}) collective-permute-start(bf16[624,256]{1,0:T(8,128)(2,1)S(1)} %collective-permute-done.25.refs_2_), channel_id=1, source_target_pairs={{0,16},{16,32},{32,48},{48,0},{64,80},{80,96},{96,112},{112,64},{1... | collective-permute-start | bytes 958472 | tf_op jit(solution)/shard_map/ppermute | solution.py:155
  101.2 11.7 %collective-permute-start.26 = (bf16[624,256]{1,0:T(8,128)(2,1)S(1)}, bf16[624,256]{1,0:T(8,128)(2,1)S(1)}, u32[]{:S(2)}, u32[]{:S(2)}) collective-permute-start(bf16[624,256]{1,0:T(8,128)(2,1)S(1)} %collective-permute-done.25.refs_2_), channel_id=1, source_target_pairs={{0,48},{16,0},{32,16},{48,32},{64,112},{80,64},{96,80},{112,96},{1... | collective-permute-start | bytes 958472 | tf_op jit(solution)/shard_map/ppermute | solution.py:155
  101.2 16.0 %collective-permute-start.30 = (bf16[624,256]{1,0:T(8,128)(2,1)S(1)}, bf16[624,256]{1,0:T(8,128)(2,1)S(1)}, u32[]{:S(2)}, u32[]{:S(2)}) collective-permute-start(bf16[624,256]{1,0:T(8,128)(2,1)S(1)} %collective-permute-done.21.refs_2_), channel_id=1, source_target_pairs={{0,64},{16,80},{32,96},{48,112},{64,128},{80,144},{96,160},{112,17... | collective-permute-start | bytes 958472 | tf_op jit(solution)/shard_map/ppermute | solution.py:155
  112.0 20.6 %collective-permute-start.36 = (bf16[1080,256]{1,0:T(8,128)(2,1)S(1)}, bf16[1080,256]{1,0:T(8,128)(2,1)S(1)}, u32[]{:S(2)}, u32[]{:S(2)}) collective-permute-start(bf16[1080,256]{1,0:T(8,128)(2,1)S(1)} %collective-permute-done.35.refs_4_.refs_5_), channel_id=1, source_target_pairs={{0,48},{16,0},{32,16},{48,32},{64,112},{80,64},{96,80},{112,96},{1... | collective-permute-start | bytes 1658888 | tf_op jit(solution)/shard_map/ppermute | solution.py:155
  112.0 22.4 %collective-permute-start.10 = (bf16[1080,256]{1,0:T(8,128)(2,1)S(1)}, bf16[1080,256]{1,0:T(8,128)(2,1)S(1)}, u32[]{:S(2)}, u32[]{:S(2)}) collective-permute-start(bf16[1080,256]{1,0:T(8,128)(2,1)S(1)} %collective-permute-done.9.refs_4_), channel_id=1, source_target_pairs={{0,192},{16,208},{32,224},{48,240},{64,0},{80,16},{96,32},{112,48}... | collective-permute-start | bytes 1658888 | tf_op jit(solution)/shard_map/ppermute | solution.py:155
  120.0 12.1 %collective-permute-start.27 = (bf16[624,256]{1,0:T(8,128)(2,1)S(1)}, bf16[624,256]{1,0:T(8,128)(2,1)S(1)}, u32[]{:S(2)}, u32[]{:S(2)}) collective-permute-start(bf16[624,256]{1,0:T(8,128)(2,1)S(1)} %collective-permute-done.26.refs_2_), channel_id=1, source_target_pairs={{0,48},{16,0},{32,16},{48,32},{64,112},{80,64},{96,80},{112,96},{1... | collective-permute-start | bytes 958472 | tf_op jit(solution)/shard_map/ppermute | solution.py:155
  121.2 27.2 %collective-permute-start.23 = (bf16[624,256]{1,0:T(8,128)(2,1)S(1)}, bf16[624,256]{1,0:T(8,128)(2,1)S(1)}, u32[]{:S(2)}, u32[]{:S(2)}) collective-permute-start(bf16[624,256]{1,0:T(8,128)(2,1)S(1)} %collective-permute-done.22.refs_2_), channel_id=1, source_target_pairs={{0,192},{16,208},{32,224},{48,240},{64,0},{80,16},{96,32},{112,48}... | collective-permute-start | bytes 958472 | tf_op jit(solution)/shard_map/ppermute | solution.py:155
  124.2 25.4 %collective-permute-start.17 = (bf16[456,256]{1,0:T(8,128)(2,1)S(1)}, bf16[456,256]{1,0:T(8,128)(2,1)S(1)}, u32[]{:S(2)}, u32[]{:S(2)}) collective-permute-start(bf16[456,256]{1,0:T(8,128)(2,1)S(1)} %collective-permute-done.16.refs_3_.refs_9_), channel_id=1, source_target_pairs={{0,48},{16,0},{32,16},{48,32},{64,112},{80,64},{96,80},{112,96},{1... | collective-permute-start | bytes 700424 | tf_op jit(solution)/shard_map/ppermute | solution.py:155
  132.1 17.5 %collective-permute-start.6 = (bf16[456,256]{1,0:T(8,128)(2,1)S(1)}, bf16[456,256]{1,0:T(8,128)(2,1)S(1)}, u32[]{:S(2)}, u32[]{:S(2)}) collective-permute-start(bf16[456,256]{1,0:T(8,128)(2,1)S(1)} %collective-permute-done.5.refs_3_), channel_id=1, source_target_pairs={{0,192},{16,208},{32,224},{48,240},{64,0},{80,16},{96,32},{112,48}... | collective-permute-start | bytes 700424 | tf_op jit(solution)/shard_map/ppermute | solution.py:155
  132.6 16.9 %collective-permute-start.13 = (bf16[456,256]{1,0:T(8,128)(2,1)S(1)}, bf16[456,256]{1,0:T(8,128)(2,1)S(1)}, u32[]{:S(2)}, u32[]{:S(2)}) collective-permute-start(bf16[456,256]{1,0:T(8,128)(2,1)S(1)} %slice.42), channel_id=1, source_target_pairs={{0,16},{16,32},{32,48},{48,0},{64,80},{80,96},{96,112},{112,64},{1... | collective-permute-start | bytes 700424 | tf_op jit(solution)/shard_map/ppermute | solution.py:155
  134.4 15.2 %collective-permute-start.2 = (bf16[456,256]{1,0:T(8,128)(2,1)S(1)}, bf16[456,256]{1,0:T(8,128)(2,1)S(1)}, u32[]{:S(2)}, u32[]{:S(2)}) collective-permute-start(bf16[456,256]{1,0:T(8,128)(2,1)S(1)} %slice.40), channel_id=1, source_target_pairs={{0,64},{16,80},{32,96},{48,112},{64,128},{80,144},{96,160},{112,17... | collective-permute-start | bytes 700424 | tf_op jit(solution)/shard_map/ppermute | solution.py:155
  (8 other events, 75.9 us)

commit v3 on v2

--- a/solution.py
+++ b/solution.py
@@ -18,6 +18,7 @@
 HALF = 64
 QUART = COLS // 4
 PIECE = COLS + QUART
+LAST = 624
 CUT = 624
 SIDE = 4
 
@@ -30,14 +31,14 @@
     for at in range(0, COLS, 128):
         n = min(128, COLS - at)
         w = w_ref[pl.ds(full_at, FULL), at : at + n] / factor[:, at : at + n]
-        o_ref[at : at + n, :] = w.T.astype(jnp.bfloat16)
+        o_ref[QUART + at : QUART + at + n, :] = w.T.astype(jnp.bfloat16)
     h = w_ref[pl.ds(half_at, HALF), :] / factor
     t = jnp.concatenate([h, h], axis=0).T
     low = lax.broadcasted_iota(jnp.int32, (2 * QUART, 128), 1) < HALF
     keep = jnp.logical_xor(low, odd == 1)
     p = jnp.where(keep, t[: 2 * QUART], t[2 * QUART :]).astype(jnp.bfloat16)
-    o_ref[COLS:, :128] = p[:QUART]
-    o_ref[COLS:, 128:] = p[QUART:]
+    o_ref[:QUART, :128] = p[:QUART]
+    o_ref[:QUART, 128:] = p[QUART:]
 
 
 def packed(w, tops, m):
@@ -74,10 +75,12 @@
         for key, part in fulls:
             at = tile_of(*key)
             for r, a, b in [layout[key, q] for q in part]:
-                hi = min(b, COLS)
-                if hi > a:
+                lo = max(a, QUART)
+                if b > lo:
                     c = pltpu.make_async_copy(
-                        ins[r].at[pl.ds(0, hi - a), :], out.at[pl.ds(a, hi - a), pl.ds(at, FULL)], sem_full.at[len(done)]
+                        ins[r].at[pl.ds(lo - a, b - lo), :],
+                        out.at[pl.ds(lo - QUART, b - lo), pl.ds(at, FULL)],
+                        sem_full.at[len(done)],
                     )
                     c.start()
                     done.append(c)
@@ -87,8 +90,7 @@
     for (layout, _, pairs), out in zip(plan, outs):
 
         def half(key, lanes):
-            r, a, _ = layout[key, -1]
-            return ins[r][COLS - a : PIECE - a, lanes].astype(jnp.float32)
+            return ins[layout[key, 0][0]][:QUART, lanes].astype(jnp.float32)
 
         for p, ky in pairs:
             tile = tiles.at[n_tiles]
@@ -117,7 +119,7 @@
     for _, got, fulls, pairs in jobs:
         layout = {}
         need = [(key, q) for key, part in fulls for q in part]
-        need += [((k, ky), -1) for p, ky in pairs for k in (2 * p, 1, 3)]
+        need += [((k, ky), 0) for p, ky in pairs for k in (2 * p, 1, 3)]
         for key, q in need:
             parts = got[key]
             one = parts[q]
@@ -216,11 +218,11 @@
         "Pu1": [("u", [(1, k) for k in every], [])],
         "Pu3": [("u", [(3, k) for k in every], [(0, k) for k in every])],
         "Pu2": [("u", [(2, 0), (2, 3)], [(1, 0), (1, 3)])],
-        "Pmid": [("g", [(1, 2), (2, 2)], []), ("u", [(2, 1), (2, 2)], [])],
-        "Pend": [
+        "Pmid": [
             ("g", [(1, 2), (2, 2)], [(0, 2), (1, 2)]),
             ("u", [(2, 1), (2, 2)], [(1, 1), (1, 2)]),
         ],
+        "Pend": [("g", [(1, 2), (2, 2)], []), ("u", [(2, 1), (2, 2)], [])],
     }
     for name in ORDER:
         if name[0] == "P":
@@ -237,9 +239,9 @@
         elif kind == "b":
             large[m][(step, q)] = move(small[m][q], on_x, sign)
         elif q == "1a":
-            large[m][(2, q)] = move(large[m][(step, "1")][:CUT], on_x, sign)
+            large[m][(2, q)] = move(large[m][(step, "1")][:LAST], on_x, sign)
         elif q == "1b":
-            large[m][(2, q)] = move(large[m][(step, "1")][CUT:], on_x, sign)
+            large[m][(2, q)] = move(large[m][(step, "1")][LAST:], on_x, sign)
         else:
             large[m][(2, q)] = move(large[m][(step, q)], on_x, sign)
     return out["g"], out["u"]

time: 151 us -> 149 us (0.987)
  waiting for transfers between devices: 73.9 us -> 72.3 us
    ppermute x40, waiting for transfers between devices: 73.9 us -> 72.3 us  [shift(): return lax.ppermute(a, 'zero', pairs)]
where the time goes in v3:
time: 149 us
  waiting for transfers between devices  72.3 us (49%)
  starting transfers between devices  46.8 us (31%)
  Pallas kernels  13.4 us (9%)
  blocking collectives  11.1 us (7%)
  other arithmetic  4.2 us (3%)
    ppermute x40, waiting for transfers between devices, shift(): return lax.ppermute(a, 'zero', pairs)  72.3 us
    ppermute x40, starting transfers between devices, shift(): return lax.ppermute(a, 'zero', pairs)  46.8 us
    pallas_call x10, Pallas kernels, place(): pl.pallas_call(functools.partial(place_kernel, plan, len(refs), first), o...  12.9 us
    all_to_all x1, blocking collectives, body(): lax.all_to_all(jnp.broadcast_to(tops, (SIDE * SIDE, 2, COLS)), 'zero', 0,...  11.1 us
    reduce_max x1, other arithmetic, body(): jnp.max(jnp.abs(gained_up), axis=0)  3.49 us
  transfers between devices with their start and end apart: 40, of which 17 were waited for; matrix products, arithmetic and copies ran while one was open for 1% of the time, Pallas kernels for 8%

profile of v3, /device:TPU:30, one launch (start us, length us, event | category | flops | bytes accessed | tf_op | source)
XLA Modules:
  0.0 149.2 jit_solution(18146957774155949133)
XLA Ops:
  0.6 3.5 %abs_reduce_fusion = (f32[864]{0:T(1024)S(1)}, f32[320,864]{1,0:T(8,128)S(1)}, f32[864]{0:T(1024)S(1)}, f32[320,864]{1,0:T(8,128)S(1)}) fusion(f32[320]{0:T(512)} %param.13, f32[320,864]{1,0:T(8,128)} %param.10, f32[320,864]{1,0:T(8,128)} %param.12, f32[320,864]{1,0:T(8,128)} %param.11, f32[320,864]{1,0:T(8,128)} %param.7, f32[320,864]{1,0:T(8,128)} %param.9, ...), kind=kLoop, calls=%fused_computation | loop fusion | flops 3868992 | bytes 8855552 | tf_op jit(solution)/shard_map/reduce_max | solution.py:257
  4.2 11.1 %all_to_all.5.tops_ref = f32[16,2,864]{2,1,0:T(2,128)S(1)} all-to-all(f32[16,2,864]{2,1,0:T(2,128)S(1)} %broadcast_in_dim.2), channel_id=1, replica_groups=mesh['zero'=16,'width'=16] {'zero'}, dimensions={0} | all-to-all | bytes 221184 | tf_op jit(solution)/shard_map/all_to_all | solution.py:258
  16.3 2.6 %collective-permute-start.18 = (bf16[1080,256]{1,0:T(8,128)(2,1)S(1)}, bf16[1080,256]{1,0:T(8,128)(2,1)S(1)}, u32[]{:S(2)}, u32[]{:S(2)}) collective-permute-start(bf16[1080,256]{1,0:T(8,128)(2,1)S(1)} %shard_map.102.refs_0_), channel_id=1, source_target_pairs={{0,64},{16,80},{32,96},{48,112},{64,128},{80,144},{96,160},{112,17... | collective-permute-start | bytes 1658888 | tf_op jit(solution)/shard_map/ppermute | solution.py:157
  19.7 2.4 %collective-permute-start = (bf16[1080,256]{1,0:T(8,128)(2,1)S(1)}, bf16[1080,256]{1,0:T(8,128)(2,1)S(1)}, u32[]{:S(2)}, u32[]{:S(2)}) collective-permute-start(bf16[1080,256]{1,0:T(8,128)(2,1)S(1)} %shard_map.102.refs_0_), channel_id=1, source_target_pairs={{0,16},{16,32},{32,48},{48,0},{64,80},{80,96},{96,112},{112,64},{1... | collective-permute-start | bytes 1658888 | tf_op jit(solution)/shard_map/ppermute | solution.py:157
  22.5 9.8 %collective-permute-done.28.refs_0_ = bf16[1080,256]{1,0:T(8,128)(2,1)S(1)} collective-permute-done((bf16[1080,256]{1,0:T(8,128)(2,1)S(1)}, bf16[1080,256]{1,0:T(8,128)(2,1)S(1)}, u32[]{:S(2)}, u32[]{:S(2)}) %collective-permute-start.28) | collective-permute-done | bytes 552992 | tf_op jit(solution)/shard_map/ppermute | solution.py:157
  34.0 2.4 %collective-permute-start.33 = (bf16[1080,256]{1,0:T(8,128)(2,1)S(1)}, bf16[1080,256]{1,0:T(8,128)(2,1)S(1)}, u32[]{:S(2)}, u32[]{:S(2)}) collective-permute-start(bf16[1080,256]{1,0:T(8,128)(2,1)S(1)} %shard_map.103.refs_0_.refs_5_), channel_id=1, source_target_pairs={{0,16},{16,32},{32,48},{48,0},{64,80},{80,96},{96,112},{112,64},{1... | collective-permute-start | bytes 1658888 | tf_op jit(solution)/shard_map/ppermute | solution.py:157
  36.6 5.0 %collective-permute-done.10.refs_4_.refs_11_ = bf16[1080,256]{1,0:T(8,128)(2,1)S(1)} collective-permute-done((bf16[1080,256]{1,0:T(8,128)(2,1)S(1)}, bf16[1080,256]{1,0:T(8,128)(2,1)S(1)}, u32[]{:S(2)}, u32[]{:S(2)}) %collective-permute-start.10) | collective-permute-done | bytes 552992 | tf_op jit(solution)/shard_map/ppermute | solution.py:157
  41.6 2.0 %collective-permute-start.15 = (bf16[624,256]{1,0:T(8,128)(2,1)S(1)}, bf16[624,256]{1,0:T(8,128)(2,1)S(1)}, u32[]{:S(2)}, u32[]{:S(2)}) collective-permute-start(bf16[624,256]{1,0:T(8,128)(2,1)S(1)} %slice.45), channel_id=1, source_target_pairs={{0,16},{16,32},{32,48},{48,0},{64,80},{80,96},{96,112},{112,64},{1... | collective-permute-start | bytes 958472 | tf_op jit(solution)/shard_map/ppermute | solution.py:157
  43.8 3.0 %collective-permute-done.37.refs_0_.refs_3_ = bf16[1080,256]{1,0:T(8,128)(2,1)S(1)} collective-permute-done((bf16[1080,256]{1,0:T(8,128)(2,1)S(1)}, bf16[1080,256]{1,0:T(8,128)(2,1)S(1)}, u32[]{:S(2)}, u32[]{:S(2)}) %collective-permute-start.37) | collective-permute-done | bytes 552992 | tf_op jit(solution)/shard_map/ppermute | solution.py:157
  53.2 1.5 %collective-permute-start.19 = (bf16[1080,256]{1,0:T(8,128)(2,1)S(1)}, bf16[1080,256]{1,0:T(8,128)(2,1)S(1)}, u32[]{:S(2)}, u32[]{:S(2)}) collective-permute-start(bf16[1080,256]{1,0:T(8,128)(2,1)S(1)} %collective-permute-done.18.refs_0_), channel_id=1, source_target_pairs={{0,64},{16,80},{32,96},{48,112},{64,128},{80,144},{96,160},{112,17... | collective-permute-start | bytes 1658888 | tf_op jit(solution)/shard_map/ppermute | solution.py:157
  54.7 1.5 %collective-permute-done.23.refs_2_.refs_9_ = bf16[624,256]{1,0:T(8,128)(2,1)S(1)} collective-permute-done((bf16[624,256]{1,0:T(8,128)(2,1)S(1)}, bf16[624,256]{1,0:T(8,128)(2,1)S(1)}, u32[]{:S(2)}, u32[]{:S(2)}) %collective-permute-start.23) | collective-permute-done | bytes 319520 | tf_op jit(solution)/shard_map/ppermute | solution.py:157
  56.2 5.0 %collective-permute-done.31.refs_3_ = bf16[456,256]{1,0:T(8,128)(2,1)S(1)} collective-permute-done((bf16[456,256]{1,0:T(8,128)(2,1)S(1)}, bf16[456,256]{1,0:T(8,128)(2,1)S(1)}, u32[]{:S(2)}, u32[]{:S(2)}) %collective-permute-start.31) | collective-permute-done | bytes 233504 | tf_op jit(solution)/shard_map/ppermute | solution.py:157
  61.2 3.5 %collective-permute-start.32 = (bf16[1080,256]{1,0:T(8,128)(2,1)S(1)}, bf16[1080,256]{1,0:T(8,128)(2,1)S(1)}, u32[]{:S(2)}, u32[]{:S(2)}) collective-permute-start(bf16[1080,256]{1,0:T(8,128)(2,1)S(1)} %collective-permute-done.3.refs_4_), channel_id=1, source_target_pairs={{0,64},{16,80},{32,96},{48,112},{64,128},{80,144},{96,160},{112,17... | collective-permute-start | bytes 1658888 | tf_op jit(solution)/shard_map/ppermute | solution.py:157
  64.9 3.2 %collective-permute-start.1 = (bf16[1080,256]{1,0:T(8,128)(2,1)S(1)}, bf16[1080,256]{1,0:T(8,128)(2,1)S(1)}, u32[]{:S(2)}, u32[]{:S(2)}) collective-permute-start(bf16[1080,256]{1,0:T(8,128)(2,1)S(1)} %collective-permute-done.refs_1_), channel_id=1, source_target_pairs={{0,64},{16,80},{32,96},{48,112},{64,128},{80,144},{96,160},{112,17... | collective-permute-start | bytes 1658888 | tf_op jit(solution)/shard_map/ppermute | solution.py:157
  68.1 5.0 %collective-permute-done.19.refs_0_.refs_2_ = bf16[1080,256]{1,0:T(8,128)(2,1)S(1)} collective-permute-done((bf16[1080,256]{1,0:T(8,128)(2,1)S(1)}, bf16[1080,256]{1,0:T(8,128)(2,1)S(1)}, u32[]{:S(2)}, u32[]{:S(2)}) %collective-permute-start.19) | collective-permute-done | bytes 552992 | tf_op jit(solution)/shard_map/ppermute | solution.py:157
  73.1 11.8 %collective-permute-done.32.refs_4_ = bf16[1080,256]{1,0:T(8,128)(2,1)S(1)} collective-permute-done((bf16[1080,256]{1,0:T(8,128)(2,1)S(1)}, bf16[1080,256]{1,0:T(8,128)(2,1)S(1)}, u32[]{:S(2)}, u32[]{:S(2)}) %collective-permute-start.32) | collective-permute-done | bytes 552992 | tf_op jit(solution)/shard_map/ppermute | solution.py:157
  85.0 2.0 %collective-permute-start.35 = (bf16[1080,256]{1,0:T(8,128)(2,1)S(1)}, bf16[1080,256]{1,0:T(8,128)(2,1)S(1)}, u32[]{:S(2)}, u32[]{:S(2)}) collective-permute-start(bf16[1080,256]{1,0:T(8,128)(2,1)S(1)} %collective-permute-done.10.refs_4_.refs_11_), channel_id=1, source_target_pairs={{0,48},{16,0},{32,16},{48,32},{64,112},{80,64},{96,80},{112,96},{1... | collective-permute-start | bytes 1658888 | tf_op jit(solution)/shard_map/ppermute | solution.py:157
  87.1 4.8 %collective-permute-done.1.refs_1_ = bf16[1080,256]{1,0:T(8,128)(2,1)S(1)} collective-permute-done((bf16[1080,256]{1,0:T(8,128)(2,1)S(1)}, bf16[1080,256]{1,0:T(8,128)(2,1)S(1)}, u32[]{:S(2)}, u32[]{:S(2)}) %collective-permute-start.1) | collective-permute-done | bytes 552992 | tf_op jit(solution)/shard_map/ppermute | solution.py:157
  92.6 3.6 %collective-permute-start.30 = (bf16[624,256]{1,0:T(8,128)(2,1)S(1)}, bf16[624,256]{1,0:T(8,128)(2,1)S(1)}, u32[]{:S(2)}, u32[]{:S(2)}) collective-permute-start(bf16[624,256]{1,0:T(8,128)(2,1)S(1)} %collective-permute-done.15.refs_2_), channel_id=1, source_target_pairs={{0,64},{16,80},{32,96},{48,112},{64,128},{80,144},{96,160},{112,17... | collective-permute-start | bytes 958472 | tf_op jit(solution)/shard_map/ppermute | solution.py:157
  96.3 3.0 %collective-permute-done.38.refs_4_.refs_12_ = bf16[1080,256]{1,0:T(8,128)(2,1)S(1)} collective-permute-done((bf16[1080,256]{1,0:T(8,128)(2,1)S(1)}, bf16[1080,256]{1,0:T(8,128)(2,1)S(1)}, u32[]{:S(2)}, u32[]{:S(2)}) %collective-permute-start.38) | collective-permute-done | bytes 552992 | tf_op jit(solution)/shard_map/ppermute | solution.py:157
  99.3 2.3 %collective-permute-start.16 = (bf16[624,256]{1,0:T(8,128)(2,1)S(1)}, bf16[624,256]{1,0:T(8,128)(2,1)S(1)}, u32[]{:S(2)}, u32[]{:S(2)}) collective-permute-start(bf16[624,256]{1,0:T(8,128)(2,1)S(1)} %collective-permute-done.15.refs_2_), channel_id=1, source_target_pairs={{0,192},{16,208},{32,224},{48,240},{64,0},{80,16},{96,32},{112,48}... | collective-permute-start | bytes 958472 | tf_op jit(solution)/shard_map/ppermute | solution.py:157
  101.6 7.9 %collective-permute-done.26.refs_1_.refs_7_ = bf16[1080,256]{1,0:T(8,128)(2,1)S(1)} collective-permute-done((bf16[1080,256]{1,0:T(8,128)(2,1)S(1)}, bf16[1080,256]{1,0:T(8,128)(2,1)S(1)}, u32[]{:S(2)}, u32[]{:S(2)}) %collective-permute-start.26) | collective-permute-done | bytes 552992 | tf_op jit(solution)/shard_map/ppermute | solution.py:157
  110.4 3.0 %collective-permute-start.14 = (bf16[624,256]{1,0:T(8,128)(2,1)S(1)}, bf16[624,256]{1,0:T(8,128)(2,1)S(1)}, u32[]{:S(2)}, u32[]{:S(2)}) collective-permute-start(bf16[624,256]{1,0:T(8,128)(2,1)S(1)} %slice.44), channel_id=1, source_target_pairs={{0,64},{16,80},{32,96},{48,112},{64,128},{80,144},{96,160},{112,17... | collective-permute-start | bytes 958472 | tf_op jit(solution)/shard_map/ppermute | solution.py:157
  114.6 2.1 %collective-permute-start.22 = (bf16[624,256]{1,0:T(8,128)(2,1)S(1)}, bf16[624,256]{1,0:T(8,128)(2,1)S(1)}, u32[]{:S(2)}, u32[]{:S(2)}) collective-permute-start(bf16[624,256]{1,0:T(8,128)(2,1)S(1)} %slice.46), channel_id=1, source_target_pairs={{0,16},{16,32},{32,48},{48,0},{64,80},{80,96},{96,112},{112,64},{1... | collective-permute-start | bytes 958472 | tf_op jit(solution)/shard_map/ppermute | solution.py:157
  116.7 3.6 %collective-permute-done.24.refs_2_.refs_9_ = bf16[624,256]{1,0:T(8,128)(2,1)S(1)} collective-permute-done((bf16[624,256]{1,0:T(8,128)(2,1)S(1)}, bf16[624,256]{1,0:T(8,128)(2,1)S(1)}, u32[]{:S(2)}, u32[]{:S(2)}) %collective-permute-start.24) | collective-permute-done | bytes 319520 | tf_op jit(solution)/shard_map/ppermute | solution.py:157
  121.6 1.6 %collective-permute-start.6 = (bf16[456,256]{1,0:T(8,128)(2,1)S(1)}, bf16[456,256]{1,0:T(8,128)(2,1)S(1)}, u32[]{:S(2)}, u32[]{:S(2)}) collective-permute-start(bf16[456,256]{1,0:T(8,128)(2,1)S(1)} %collective-permute-done.5.refs_3_), channel_id=1, source_target_pairs={{0,192},{16,208},{32,224},{48,240},{64,0},{80,16},{96,32},{112,48}... | collective-permute-start | bytes 700424 | tf_op jit(solution)/shard_map/ppermute | solution.py:157
  123.2 6.8 %collective-permute-done.17.refs_1_ = bf16[624,256]{1,0:T(8,128)(2,1)S(1)} collective-permute-done((bf16[624,256]{1,0:T(8,128)(2,1)S(1)}, bf16[624,256]{1,0:T(8,128)(2,1)S(1)}, u32[]{:S(2)}, u32[]{:S(2)}) %collective-permute-start.17) | collective-permute-done | bytes 319520 | tf_op jit(solution)/shard_map/ppermute | solution.py:157
  130.0 2.0 %collective-permute-start.2 = (bf16[456,256]{1,0:T(8,128)(2,1)S(1)}, bf16[456,256]{1,0:T(8,128)(2,1)S(1)}, u32[]{:S(2)}, u32[]{:S(2)}) collective-permute-start(bf16[456,256]{1,0:T(8,128)(2,1)S(1)} %slice.40), channel_id=1, source_target_pairs={{0,64},{16,80},{32,96},{48,112},{64,128},{80,144},{96,160},{112,17... | collective-permute-start | bytes 700424 | tf_op jit(solution)/shard_map/ppermute | solution.py:157
  132.1 3.2 %collective-permute-start.9 = (bf16[456,256]{1,0:T(8,128)(2,1)S(1)}, bf16[456,256]{1,0:T(8,128)(2,1)S(1)}, u32[]{:S(2)}, u32[]{:S(2)}) collective-permute-start(bf16[456,256]{1,0:T(8,128)(2,1)S(1)} %slice.42), channel_id=1, source_target_pairs={{0,16},{16,32},{32,48},{48,0},{64,80},{80,96},{96,112},{112,64},{1... | collective-permute-start | bytes 700424 | tf_op jit(solution)/shard_map/ppermute | solution.py:157
  138.7 1.4 shard_map.105.refs_5_
  140.2 1.4 shard_map.106.refs_2_
  142.9 1.6 %shard_map.110.refs_6_ = bf16[864,5120]{1,0:T(8,128)(2,1)} custom-call(bf16[1080,256]{1,0:T(8,128)(2,1)S(1)} %collective-permute-done.37.refs_0_.refs_3_, bf16[1080,256]{1,0:T(8,128)(2,1)S(1)} %collective-permute-done.26.refs_1_.refs_7_, bf16[624,256]{1,0:T(8,128)(2,1)S(1)} %collective-permute-done.24.refs_2_.refs_9_, ...), custom_call_target="tpu_custom_call", output_to_operand_aliasing={{}: (13, {})} | custom-call | flops 1000000 | bytes 4000000 | tf_op jit(solution)/shard_map/pallas_call | solution.py:137
  (75 shorter events, 23.9 us)
Async XLA Ops:
  15.6 16.7 %collective-permute-start.28 = (bf16[1080,256]{1,0:T(8,128)(2,1)S(1)}, bf16[1080,256]{1,0:T(8,128)(2,1)S(1)}, u32[]{:S(2)}, u32[]{:S(2)}) collective-permute-start(bf16[1080,256]{1,0:T(8,128)(2,1)S(1)} %shard_map.102.refs_0_), channel_id=1, source_target_pairs={{0,192},{16,208},{32,224},{48,240},{64,0},{80,16},{96,32},{112,48}... | collective-permute-start | bytes 1658888 | tf_op jit(solution)/shard_map/ppermute | solution.py:157
  16.3 16.8 %collective-permute-start.18 = (bf16[1080,256]{1,0:T(8,128)(2,1)S(1)}, bf16[1080,256]{1,0:T(8,128)(2,1)S(1)}, u32[]{:S(2)}, u32[]{:S(2)}) collective-permute-start(bf16[1080,256]{1,0:T(8,128)(2,1)S(1)} %shard_map.102.refs_0_), channel_id=1, source_target_pairs={{0,64},{16,80},{32,96},{48,112},{64,128},{80,144},{96,160},{112,17... | collective-permute-start | bytes 1658888 | tf_op jit(solution)/shard_map/ppermute | solution.py:157
  18.9 15.0 %collective-permute-start.3 = (bf16[1080,256]{1,0:T(8,128)(2,1)S(1)}, bf16[1080,256]{1,0:T(8,128)(2,1)S(1)}, u32[]{:S(2)}, u32[]{:S(2)}) collective-permute-start(bf16[1080,256]{1,0:T(8,128)(2,1)S(1)} %shard_map.102.refs_0_), channel_id=1, source_target_pairs={{0,48},{16,0},{32,16},{48,32},{64,112},{80,64},{96,80},{112,96},{1... | collective-permute-start | bytes 1658888 | tf_op jit(solution)/shard_map/ppermute | solution.py:157
  19.7 16.7 %collective-permute-start = (bf16[1080,256]{1,0:T(8,128)(2,1)S(1)}, bf16[1080,256]{1,0:T(8,128)(2,1)S(1)}, u32[]{:S(2)}, u32[]{:S(2)}) collective-permute-start(bf16[1080,256]{1,0:T(8,128)(2,1)S(1)} %shard_map.102.refs_0_), channel_id=1, source_target_pairs={{0,16},{16,32},{32,48},{48,0},{64,80},{80,96},{96,112},{112,64},{1... | collective-permute-start | bytes 1658888 | tf_op jit(solution)/shard_map/ppermute | solution.py:157
  22.5 19.2 %collective-permute-start.10 = (bf16[1080,256]{1,0:T(8,128)(2,1)S(1)}, bf16[1080,256]{1,0:T(8,128)(2,1)S(1)}, u32[]{:S(2)}, u32[]{:S(2)}) collective-permute-start(bf16[1080,256]{1,0:T(8,128)(2,1)S(1)} %shard_map.103.refs_0_.refs_5_), channel_id=1, source_target_pairs={{0,192},{16,208},{32,224},{48,240},{64,0},{80,16},{96,32},{112,48}... | collective-permute-start | bytes 1658888 | tf_op jit(solution)/shard_map/ppermute | solution.py:157
  32.3 11.3 %collective-permute-start.7 = (bf16[1080,256]{1,0:T(8,128)(2,1)S(1)}, bf16[1080,256]{1,0:T(8,128)(2,1)S(1)}, u32[]{:S(2)}, u32[]{:S(2)}) collective-permute-start(bf16[1080,256]{1,0:T(8,128)(2,1)S(1)} %shard_map.103.refs_0_.refs_5_), channel_id=1, source_target_pairs={{0,64},{16,80},{32,96},{48,112},{64,128},{80,144},{96,160},{112,17... | collective-permute-start | bytes 1658888 | tf_op jit(solution)/shard_map/ppermute | solution.py:157
  33.2 13.6 %collective-permute-start.37 = (bf16[1080,256]{1,0:T(8,128)(2,1)S(1)}, bf16[1080,256]{1,0:T(8,128)(2,1)S(1)}, u32[]{:S(2)}, u32[]{:S(2)}) collective-permute-start(bf16[1080,256]{1,0:T(8,128)(2,1)S(1)} %shard_map.103.refs_0_.refs_5_), channel_id=1, source_target_pairs={{0,48},{16,0},{32,16},{48,32},{64,112},{80,64},{96,80},{112,96},{1... | collective-permute-start | bytes 1658888 | tf_op jit(solution)/shard_map/ppermute | solution.py:157
  34.0 16.7 %collective-permute-start.33 = (bf16[1080,256]{1,0:T(8,128)(2,1)S(1)}, bf16[1080,256]{1,0:T(8,128)(2,1)S(1)}, u32[]{:S(2)}, u32[]{:S(2)}) collective-permute-start(bf16[1080,256]{1,0:T(8,128)(2,1)S(1)} %shard_map.103.refs_0_.refs_5_), channel_id=1, source_target_pairs={{0,16},{16,32},{32,48},{48,0},{64,80},{80,96},{96,112},{112,64},{1... | collective-permute-start | bytes 1658888 | tf_op jit(solution)/shard_map/ppermute | solution.py:157
  36.5 12.8 %collective-permute-start.4 = (bf16[456,256]{1,0:T(8,128)(2,1)S(1)}, bf16[456,256]{1,0:T(8,128)(2,1)S(1)}, u32[]{:S(2)}, u32[]{:S(2)}) collective-permute-start(bf16[456,256]{1,0:T(8,128)(2,1)S(1)} %slice.41), channel_id=1, source_target_pairs={{0,48},{16,0},{32,16},{48,32},{64,112},{80,64},{96,80},{112,96},{1... | collective-permute-start | bytes 700424 | tf_op jit(solution)/shard_map/ppermute | solution.py:157
  41.6 11.6 %collective-permute-start.15 = (bf16[624,256]{1,0:T(8,128)(2,1)S(1)}, bf16[624,256]{1,0:T(8,128)(2,1)S(1)}, u32[]{:S(2)}, u32[]{:S(2)}) collective-permute-start(bf16[624,256]{1,0:T(8,128)(2,1)S(1)} %slice.45), channel_id=1, source_target_pairs={{0,16},{16,32},{32,48},{48,0},{64,80},{80,96},{96,112},{112,64},{1... | collective-permute-start | bytes 958472 | tf_op jit(solution)/shard_map/ppermute | solution.py:157
  49.3 12.0 %collective-permute-start.31 = (bf16[456,256]{1,0:T(8,128)(2,1)S(1)}, bf16[456,256]{1,0:T(8,128)(2,1)S(1)}, u32[]{:S(2)}, u32[]{:S(2)}) collective-permute-start(bf16[456,256]{1,0:T(8,128)(2,1)S(1)} %collective-permute-done.4.refs_3_), channel_id=1, source_target_pairs={{0,64},{16,80},{32,96},{48,112},{64,128},{80,144},{96,160},{112,17... | collective-permute-start | bytes 700424 | tf_op jit(solution)/shard_map/ppermute | solution.py:157
  50.6 14.1 %collective-permute-start.5 = (bf16[456,256]{1,0:T(8,128)(2,1)S(1)}, bf16[456,256]{1,0:T(8,128)(2,1)S(1)}, u32[]{:S(2)}, u32[]{:S(2)}) collective-permute-start(bf16[456,256]{1,0:T(8,128)(2,1)S(1)} %collective-permute-done.4.refs_3_), channel_id=1, source_target_pairs={{0,192},{16,208},{32,224},{48,240},{64,0},{80,16},{96,32},{112,48}... | collective-permute-start | bytes 700424 | tf_op jit(solution)/shard_map/ppermute | solution.py:157
  52.5 12.3 %collective-permute-start.39 = (bf16[456,256]{1,0:T(8,128)(2,1)S(1)}, bf16[456,256]{1,0:T(8,128)(2,1)S(1)}, u32[]{:S(2)}, u32[]{:S(2)}) collective-permute-start(bf16[456,256]{1,0:T(8,128)(2,1)S(1)} %collective-permute-done.11.refs_3_), channel_id=1, source_target_pairs={{0,16},{16,32},{32,48},{48,0},{64,80},{80,96},{96,112},{112,64},{1... | collective-permute-start | bytes 700424 | tf_op jit(solution)/shard_map/ppermute | solution.py:157
  53.2 19.9 %collective-permute-start.19 = (bf16[1080,256]{1,0:T(8,128)(2,1)S(1)}, bf16[1080,256]{1,0:T(8,128)(2,1)S(1)}, u32[]{:S(2)}, u32[]{:S(2)}) collective-permute-start(bf16[1080,256]{1,0:T(8,128)(2,1)S(1)} %collective-permute-done.18.refs_0_), channel_id=1, source_target_pairs={{0,64},{16,80},{32,96},{48,112},{64,128},{80,144},{96,160},{112,17... | collective-permute-start | bytes 1658888 | tf_op jit(solution)/shard_map/ppermute | solution.py:157
  61.2 23.7 %collective-permute-start.32 = (bf16[1080,256]{1,0:T(8,128)(2,1)S(1)}, bf16[1080,256]{1,0:T(8,128)(2,1)S(1)}, u32[]{:S(2)}, u32[]{:S(2)}) collective-permute-start(bf16[1080,256]{1,0:T(8,128)(2,1)S(1)} %collective-permute-done.3.refs_4_), channel_id=1, source_target_pairs={{0,64},{16,80},{32,96},{48,112},{64,128},{80,144},{96,160},{112,17... | collective-permute-start | bytes 1658888 | tf_op jit(solution)/shard_map/ppermute | solution.py:157
  64.8 20.2 %collective-permute-start.20 = (bf16[1080,256]{1,0:T(8,128)(2,1)S(1)}, bf16[1080,256]{1,0:T(8,128)(2,1)S(1)}, u32[]{:S(2)}, u32[]{:S(2)}) collective-permute-start(bf16[1080,256]{1,0:T(8,128)(2,1)S(1)} %collective-permute-done.3.refs_4_), channel_id=1, source_target_pairs={{0,192},{16,208},{32,224},{48,240},{64,0},{80,16},{96,32},{112,48}... | collective-permute-start | bytes 1658888 | tf_op jit(solution)/shard_map/ppermute | solution.py:157
  64.8 22.2 %collective-permute-start.29 = (bf16[1080,256]{1,0:T(8,128)(2,1)S(1)}, bf16[1080,256]{1,0:T(8,128)(2,1)S(1)}, u32[]{:S(2)}, u32[]{:S(2)}) collective-permute-start(bf16[1080,256]{1,0:T(8,128)(2,1)S(1)} %collective-permute-done.refs_1_), channel_id=1, source_target_pairs={{0,192},{16,208},{32,224},{48,240},{64,0},{80,16},{96,32},{112,48}... | collective-permute-start | bytes 1658888 | tf_op jit(solution)/shard_map/ppermute | solution.py:157
  64.9 26.9 %collective-permute-start.1 = (bf16[1080,256]{1,0:T(8,128)(2,1)S(1)}, bf16[1080,256]{1,0:T(8,128)(2,1)S(1)}, u32[]{:S(2)}, u32[]{:S(2)}) collective-permute-start(bf16[1080,256]{1,0:T(8,128)(2,1)S(1)} %collective-permute-done.refs_1_), channel_id=1, source_target_pairs={{0,64},{16,80},{32,96},{48,112},{64,128},{80,144},{96,160},{112,17... | collective-permute-start | bytes 1658888 | tf_op jit(solution)/shard_map/ppermute | solution.py:157
  73.1 19.5 %collective-permute-start.34 = (bf16[1080,256]{1,0:T(8,128)(2,1)S(1)}, bf16[1080,256]{1,0:T(8,128)(2,1)S(1)}, u32[]{:S(2)}, u32[]{:S(2)}) collective-permute-start(bf16[1080,256]{1,0:T(8,128)(2,1)S(1)} %collective-permute-done.33.refs_0_.refs_6_.refs_2_), channel_id=1, source_target_pairs={{0,16},{16,32},{32,48},{48,0},{64,80},{80,96},{96,112},{112,64},{1... | collective-permute-start | bytes 1658888 | tf_op jit(solution)/shard_map/ppermute | solution.py:157
  84.9 14.4 %collective-permute-start.38 = (bf16[1080,256]{1,0:T(8,128)(2,1)S(1)}, bf16[1080,256]{1,0:T(8,128)(2,1)S(1)}, u32[]{:S(2)}, u32[]{:S(2)}) collective-permute-start(bf16[1080,256]{1,0:T(8,128)(2,1)S(1)} %collective-permute-done.10.refs_4_.refs_11_), channel_id=1, source_target_pairs={{0,16},{16,32},{32,48},{48,0},{64,80},{80,96},{96,112},{112,64},{1... | collective-permute-start | bytes 1658888 | tf_op jit(solution)/shard_map/ppermute | solution.py:157
  85.0 16.7 %collective-permute-start.35 = (bf16[1080,256]{1,0:T(8,128)(2,1)S(1)}, bf16[1080,256]{1,0:T(8,128)(2,1)S(1)}, u32[]{:S(2)}, u32[]{:S(2)}) collective-permute-start(bf16[1080,256]{1,0:T(8,128)(2,1)S(1)} %collective-permute-done.10.refs_4_.refs_11_), channel_id=1, source_target_pairs={{0,48},{16,0},{32,16},{48,32},{64,112},{80,64},{96,80},{112,96},{1... | collective-permute-start | bytes 1658888 | tf_op jit(solution)/shard_map/ppermute | solution.py:157
  87.0 22.5 %collective-permute-start.26 = (bf16[1080,256]{1,0:T(8,128)(2,1)S(1)}, bf16[1080,256]{1,0:T(8,128)(2,1)S(1)}, u32[]{:S(2)}, u32[]{:S(2)}) collective-permute-start(bf16[1080,256]{1,0:T(8,128)(2,1)S(1)} %collective-permute-done.7.refs_1_.refs_7_), channel_id=1, source_target_pairs={{0,48},{16,0},{32,16},{48,32},{64,112},{80,64},{96,80},{112,96},{1... | collective-permute-start | bytes 1658888 | tf_op jit(solution)/shard_map/ppermute | solution.py:157
  91.8 17.9 %collective-permute-start.8 = (bf16[1080,256]{1,0:T(8,128)(2,1)S(1)}, bf16[1080,256]{1,0:T(8,128)(2,1)S(1)}, u32[]{:S(2)}, u32[]{:S(2)}) collective-permute-start(bf16[1080,256]{1,0:T(8,128)(2,1)S(1)} %collective-permute-done.7.refs_1_.refs_7_), channel_id=1, source_target_pairs={{0,16},{16,32},{32,48},{48,0},{64,80},{80,96},{96,112},{112,64},{1... | collective-permute-start | bytes 1658888 | tf_op jit(solution)/shard_map/ppermute | solution.py:157
  92.6 17.7 %collective-permute-start.30 = (bf16[624,256]{1,0:T(8,128)(2,1)S(1)}, bf16[624,256]{1,0:T(8,128)(2,1)S(1)}, u32[]{:S(2)}, u32[]{:S(2)}) collective-permute-start(bf16[624,256]{1,0:T(8,128)(2,1)S(1)} %collective-permute-done.15.refs_2_), channel_id=1, source_target_pairs={{0,64},{16,80},{32,96},{48,112},{64,128},{80,144},{96,160},{112,17... | collective-permute-start | bytes 958472 | tf_op jit(solution)/shard_map/ppermute | solution.py:157
  101.6 13.0 %collective-permute-start.27 = (bf16[624,256]{1,0:T(8,128)(2,1)S(1)}, bf16[624,256]{1,0:T(8,128)(2,1)S(1)}, u32[]{:S(2)}, u32[]{:S(2)}) collective-permute-start(bf16[624,256]{1,0:T(8,128)(2,1)S(1)} %collective-permute-done.23.refs_2_.refs_9_), channel_id=1, source_target_pairs={{0,16},{16,32},{32,48},{48,0},{64,80},{80,96},{96,112},{112,64},{1... | collective-permute-start | bytes 958472 | tf_op jit(solution)/shard_map/ppermute | solution.py:157
  109.7 20.3 %collective-permute-start.21 = (bf16[1080,256]{1,0:T(8,128)(2,1)S(1)}, bf16[1080,256]{1,0:T(8,128)(2,1)S(1)}, u32[]{:S(2)}, u32[]{:S(2)}) collective-permute-start(bf16[1080,256]{1,0:T(8,128)(2,1)S(1)} %collective-permute-done.20.refs_4_), channel_id=1, source_target_pairs={{0,192},{16,208},{32,224},{48,240},{64,0},{80,16},{96,32},{112,48}... | collective-permute-start | bytes 1658888 | tf_op jit(solution)/shard_map/ppermute | solution.py:157
  110.3 21.7 %collective-permute-start.36 = (bf16[1080,256]{1,0:T(8,128)(2,1)S(1)}, bf16[1080,256]{1,0:T(8,128)(2,1)S(1)}, u32[]{:S(2)}, u32[]{:S(2)}) collective-permute-start(bf16[1080,256]{1,0:T(8,128)(2,1)S(1)} %collective-permute-done.35.refs_4_.refs_5_), channel_id=1, source_target_pairs={{0,48},{16,0},{32,16},{48,32},{64,112},{80,64},{96,80},{112,96},{1... | collective-permute-start | bytes 1658888 | tf_op jit(solution)/shard_map/ppermute | solution.py:157
  120.4 26.3 %collective-permute-start.25 = (bf16[624,256]{1,0:T(8,128)(2,1)S(1)}, bf16[624,256]{1,0:T(8,128)(2,1)S(1)}, u32[]{:S(2)}, u32[]{:S(2)}) collective-permute-start(bf16[624,256]{1,0:T(8,128)(2,1)S(1)} %collective-permute-done.24.refs_2_.refs_9_), channel_id=1, source_target_pairs={{0,48},{16,0},{32,16},{48,32},{64,112},{80,64},{96,80},{112,96},{1... | collective-permute-start | bytes 958472 | tf_op jit(solution)/shard_map/ppermute | solution.py:157
  121.6 26.3 %collective-permute-start.6 = (bf16[456,256]{1,0:T(8,128)(2,1)S(1)}, bf16[456,256]{1,0:T(8,128)(2,1)S(1)}, u32[]{:S(2)}, u32[]{:S(2)}) collective-permute-start(bf16[456,256]{1,0:T(8,128)(2,1)S(1)} %collective-permute-done.5.refs_3_), channel_id=1, source_target_pairs={{0,192},{16,208},{32,224},{48,240},{64,0},{80,16},{96,32},{112,48}... | collective-permute-start | bytes 700424 | tf_op jit(solution)/shard_map/ppermute | solution.py:157
  130.0 17.9 %collective-permute-start.13 = (bf16[456,256]{1,0:T(8,128)(2,1)S(1)}, bf16[456,256]{1,0:T(8,128)(2,1)S(1)}, u32[]{:S(2)}, u32[]{:S(2)}) collective-permute-start(bf16[456,256]{1,0:T(8,128)(2,1)S(1)} %collective-permute-done.12.refs_3_), channel_id=1, source_target_pairs={{0,48},{16,0},{32,16},{48,32},{64,112},{80,64},{96,80},{112,96},{1... | collective-permute-start | bytes 700424 | tf_op jit(solution)/shard_map/ppermute | solution.py:157
  130.0 17.9 %collective-permute-start.2 = (bf16[456,256]{1,0:T(8,128)(2,1)S(1)}, bf16[456,256]{1,0:T(8,128)(2,1)S(1)}, u32[]{:S(2)}, u32[]{:S(2)}) collective-permute-start(bf16[456,256]{1,0:T(8,128)(2,1)S(1)} %slice.40), channel_id=1, source_target_pairs={{0,64},{16,80},{32,96},{48,112},{64,128},{80,144},{96,160},{112,17... | collective-permute-start | bytes 700424 | tf_op jit(solution)/shard_map/ppermute | solution.py:157
  132.1 15.9 %collective-permute-start.9 = (bf16[456,256]{1,0:T(8,128)(2,1)S(1)}, bf16[456,256]{1,0:T(8,128)(2,1)S(1)}, u32[]{:S(2)}, u32[]{:S(2)}) collective-permute-start(bf16[456,256]{1,0:T(8,128)(2,1)S(1)} %slice.42), channel_id=1, source_target_pairs={{0,16},{16,32},{32,48},{48,0},{64,80},{80,96},{96,112},{112,64},{1... | collective-permute-start | bytes 700424 | tf_op jit(solution)/shard_map/ppermute | solution.py:157
  (8 other events, 75.5 us)
